TPU v7x, 128 devices: a whole 4x4x4 slice. The times are simulated.
128 devices in a mesh: group: 8 (over x_lo, y), dp: 16 (over x_hi, z, core).
Axes of the slice: x: 4 (x_hi: 2, x_lo: 2; x = x_hi * 2 + x_lo), y: 4, z: 4, core: 2. Of those that a mesh axis runs over, the one named last changes fastest.
Arguments:
- observations: bfloat16 [128, 64, 4096], P('dp', None, 'group'), may hold values from -6 to 6
- next_observations: bfloat16 [2048, 4096], P('dp', 'group'), may hold values from -6 to 6
- trunk_weights: bfloat16 [2, 4096, 4096], P(None, 'dp', 'group'), may hold values from -0.125 to 0.125
- head_weights: bfloat16 [4096, 19], P('group'), may hold values from -0.25 to 0.25
- acting_policy_logits: float32 [128, 63, 18], P('dp'), may hold values from -16 to 330, as said below
- actions: int32 [128, 63], P('dp'), may hold values from 0 to 17
- rewards: float32 [128, 63], P('dp'), may hold values from -6 to 6
- episode_finished: int32 [128, 63], P('dp'), may hold values 0 or 1
Outputs:
- trunk_grads: float32 [2, 4096, 4096], P(None, 'dp', 'group')
- head_grads: float32 [4096, 19], P(('group', 'dp'))
- actor_logits: float32 [2048, 18], P('dp')
Inputs may be any that keep to these rules, and one draw needn't show every extreme that they name: `acting_policy_logits`: Real-valued scores, one row for each step and trajectory.
All inputs are finite; a program needn't handle non-finite values. No bound on the sum of `episode_finished` on one device may be relied on, other than what follows from the above.
Results may differ from a plain program's by a relative error of at most 0.012.
Values may be sent and summed in bfloat16 or wider, within the bound.
A program may use at most 128 MiB of HBM per device.

v0:
```python
import jax
import jax.numpy as jnp
from jax import lax
from jax.sharding import Mesh
from jax.sharding import PartitionSpec as P

DP = ("dp_0", "dp_1", "dp_2")
GROUP_DP = ("group", "dp_0", "dp_1", "dp_2")


discount_rate = 0.99
value_weight = 0.5
entropy_weight = 0.1
loss_divisor = 16.0


def from_everyone(array, axis):
    size = lax.axis_size(axis)
    return lax.all_to_all(
        jnp.broadcast_to(array[None], (size, *array.shape)), axis, 0, 0, tiled=True
    )


def in_order(parts, dim):
    lengths = list(parts.shape[1:])
    lengths[dim] *= parts.shape[0]
    return jnp.moveaxis(parts, 0, dim).reshape(lengths)


def whole_of(array, axes, dim):
    far, near = axes
    parts = from_everyone(from_everyone(array, far), near)
    return in_order(parts.swapaxes(0, 1).reshape(-1, *array.shape), dim)


def of_everyone(array, axis):
    return from_everyone(array, axis).sum(axis=0)


def in_blocks(array, dim, size):
    lengths = array.shape
    parts = array.reshape(*lengths[:dim], size, lengths[dim] // size, *lengths[dim + 1 :])
    return jnp.moveaxis(parts, dim, 0)


def sum_at_owner(array, axis, dim):
    parts = in_blocks(array, dim, lax.axis_size(axis))
    arrived = lax.all_to_all(parts, axis, split_axis=0, concat_axis=0, tiled=True)
    return arrived.sum(axis=0)


def sent_and_summed(array, axis, dim):
    parts = in_blocks(array, dim, lax.axis_size(axis))
    arrived = lax.all_to_all(parts, axis, split_axis=0, concat_axis=0, tiled=True)
    return arrived.astype(jnp.float32).sum(axis=0)


def sum_in_two_steps(array, axes, dim):
    far, near = axes
    parts = in_blocks(array, dim, lax.axis_size(far))
    nearer = sent_and_summed(parts, near, dim + 1)
    arrived = lax.all_to_all(
        nearer.astype(jnp.bfloat16), far, split_axis=0, concat_axis=0, tiled=True
    )
    return arrived.astype(jnp.float32).sum(axis=0)


def contract_rows(left, right):
    return lax.dot_general(
        left, right, (((0,), (0,)), ((), ())), preferred_element_type=jnp.float32
    )


def contract_cols(left, right):
    return lax.dot_general(
        left, right, (((1,), (1,)), ((), ())), preferred_element_type=jnp.float32
    )


def silu_slope(pre_value):
    sigma = jax.nn.sigmoid(pre_value)
    return sigma * (1.0 + pre_value * (1.0 - sigma))


def importance_trace_gradients(
    learner_output, acting_policy_logits, actions, rewards, episode_finished
):
    number_of_actions = acting_policy_logits.shape[-1]
    logits = learner_output[:, :, :number_of_actions]
    values = learner_output[:, :, number_of_actions]
    log_policy = jax.nn.log_softmax(logits[:, :-1], axis=-1)
    log_behave = jax.nn.log_softmax(acting_policy_logits, axis=-1)
    chosen = (
        actions[:, :, None] == jnp.arange(number_of_actions, dtype=jnp.int32)[None, None, :]
    ).astype(jnp.float32)
    ratio = jnp.exp(jnp.sum((log_policy - log_behave) * chosen, axis=-1))
    clipped = jnp.minimum(ratio, 1.0)
    discount = discount_rate * (1.0 - episode_finished.astype(jnp.float32))
    current = values[:, :-1]
    following = values[:, 1:]
    deltas = clipped * (rewards + discount * following - current)

    def backward_step(carried, step_item):
        delta_now, factor_now = step_item
        carried = delta_now + factor_now * carried
        return (carried, carried)

    start_carry = jnp.zeros((values.shape[0],), jnp.float32)
    _, corrections = lax.scan(
        backward_step, start_carry, (deltas.T, (discount * clipped).T), reverse=True
    )
    targets = current + corrections.T
    next_targets = jnp.concatenate([targets[:, 1:], values[:, -1:]], axis=1)
    advantage = clipped * (rewards + discount * next_targets - current)
    probability = jnp.exp(log_policy)
    entropy = -jnp.sum(probability * log_policy, axis=-1)
    logit_grad = (
        -advantage[..., None] * (chosen - probability)
        + entropy_weight * probability * (log_policy + entropy[..., None])
    ) / loss_divisor
    value_grad = -value_weight * (targets - current) / loss_divisor
    step_grad = jnp.concatenate([logit_grad, value_grad[..., None]], axis=-1)
    last_row = jnp.zeros((values.shape[0], 1, number_of_actions + 1), jnp.float32)
    return jnp.concatenate([step_grad, last_row], axis=1)


def per_device(
    observations,
    next_observations,
    trunk_weights,
    head_weights,
    acting_policy_logits,
    actions,
    rewards,
    episode_finished,
):
    traj_count, step_count, feature_block = observations.shape
    learner_rows = traj_count * step_count
    number_of_actions = acting_policy_logits.shape[-1]
    layer_total = trunk_weights.shape[0]
    own_rows = observations.reshape(learner_rows, feature_block)
    gathered_weights = [
        whole_of(trunk_weights[layer_index], (("dp_0", "dp_1"), "dp_2"), 0)
        for layer_index in range(layer_total)
    ]
    joined = jnp.concatenate([own_rows, next_observations], axis=0)
    forward_inputs_full = []
    products_block = []
    current = joined
    for forward_layer_index in range(layer_total):
        forward_whole = lax.all_gather(current, "group", axis=1, tiled=True)
        forward_inputs_full.append(forward_whole)
        product = jnp.dot(
            forward_whole, gathered_weights[forward_layer_index], preferred_element_type=jnp.float32
        )
        products_block.append(product)
        current = jax.nn.silu(product).astype(jnp.bfloat16)
    partial_head = jnp.dot(current, head_weights, preferred_element_type=jnp.float32)
    totals = of_everyone(partial_head, "group")
    inputs_full, products_block, last_block, totals = (
        forward_inputs_full,
        products_block,
        current,
        totals,
    )
    inputs_full = [whole[:learner_rows] for whole in inputs_full]
    products_block = [block[:learner_rows] for block in products_block]
    last_block = last_block[:learner_rows]
    head_out = totals[:learner_rows]
    actor_logits = totals[learner_rows:, :number_of_actions]
    learner_output = head_out.reshape(traj_count, step_count, number_of_actions + 1)
    output_gradient = importance_trace_gradients(
        learner_output, acting_policy_logits, actions, rewards, episode_finished
    )
    output_gradient = output_gradient.reshape(learner_rows, number_of_actions + 1).astype(
        jnp.bfloat16
    )
    head_partial = contract_rows(last_block, output_gradient)
    head_grads = sum_at_owner(head_partial, DP, 0)
    input_grad = contract_cols(output_gradient, head_weights)
    owner_rows = feature_block * lax.axis_size("group") // lax.axis_size(DP)
    grad_list = [None] * layer_total
    for layer_index in range(layer_total - 1, -1, -1):
        pre_grad = (input_grad * silu_slope(products_block[layer_index])).astype(jnp.bfloat16)

        def grad_term(offset, amount, inputs=inputs_full[layer_index], upstream=pre_grad):
            return contract_rows(inputs, upstream)

        grad_list[layer_index] = sum_in_two_steps(
            grad_term(jnp.int32(0), owner_rows * lax.axis_size(DP)).astype(jnp.bfloat16),
            (("dp_0", "dp_1"), "dp_2"),
            0,
        )
        if layer_index > 0:
            full_grad = contract_cols(pre_grad, gathered_weights[layer_index])
            input_grad = lax.psum_scatter(
                full_grad.astype(jnp.bfloat16), "group", scatter_dimension=1, tiled=True
            ).astype(jnp.float32)
    return (jnp.stack(grad_list), head_grads, actor_logits)


def solution(mesh):
    split = Mesh(
        mesh.devices.reshape(mesh.shape["group"], 2, 4, 2), ("group", "dp_0", "dp_1", "dp_2")
    )
    return jax.shard_map(
        per_device,
        mesh=split,
        in_specs=(
            P(DP, None, "group"),
            P(DP, "group"),
            P(None, DP, "group"),
            P("group", None),
            P(DP, None, None),
            P(DP, None),
            P(DP, None),
            P(DP, None),
        ),
        out_specs=(P(None, DP, "group"), P(GROUP_DP, None), P(DP, None)),
        check_vma=False,
    )
```

profile of v0, /device:TPU:0, one launch (start us, length us, event | category | flops | bytes accessed | tf_op | source)
XLA Modules:
  0.0 364.0 jit_solution(16477046319909089404)
XLA Ops:
  7.2 0.0 all-gather.3.cloned.1.call-start
  7.2 2.0 pad_maximum_fusion.1
  9.2 0.0 all-gather.3.cloned.1.call-update
  9.2 0.0 all-gather.5.cloned.1.call-start
  9.3 1.1 slice_bitcast_fusion.1
  10.4 0.2 broadcast_in_dim.56
  10.6 56.0 %all_to_all.50 = bf16[8,256,512]{2,1,0:T(8,128)(2,1)S(1)} all-to-all(bf16[8,256,512]{2,1,0:T(8,128)(2,1)S(1)} %broadcast_in_dim.56), channel_id=1, replica_groups=mesh['group'=8,'dp_0'=2,'dp_1'=4,'dp_2'=2] {'dp_0','dp_1'}, dimensions={0} | all-to-all | bytes 4194304 | tf_op jit(solution)/shard_map/all_to_all | solution.py:19
  66.6 0.5 broadcast_in_dim.57
  67.1 7.1 %all_to_all.51 = bf16[2,8,256,512]{3,2,1,0:T(8,128)(2,1)S(1)} all-to-all(bf16[2,8,256,512]{3,2,1,0:T(8,128)(2,1)S(1)} %broadcast_in_dim.57), channel_id=1, replica_groups=mesh['group'=8,'dp_0'=2,'dp_1'=4,'dp_2'=2] {'dp_2'}, dimensions={0} | all-to-all | bytes 8388608 | tf_op jit(solution)/shard_map/all_to_all | solution.py:19
  74.2 2.4 copy.46
  76.6 17.5 %all-gather.3.cloned.1.call-done = bf16[640,4096]{1,0:T(8,128)(2,1)} async-done(((bf16[640,512]{1,0:T(8,128)(2,1)}), bf16[640,4096]{1,0:T(8,128)(2,1)}) %all-gather.3.cloned.1.call-update) | async-done | bytes 5242896 | tf_op jit(solution)/shard_map/all_gather | solution.py:151
  94.1 8.0 %multiply_convert_fusion.1 = (bf16[640,512]{1,0:T(8,128)(2,1)}, f32[640,512]{1,0:T(8,128)}) fusion(bf16[640,4096]{1,0:T(8,128)(2,1)} %all-gather.3.cloned.1.call-done, bf16[4096,512]{1,0:T(8,128)(2,1)} %bitcast.73), kind=kOutput, calls=%fused_computation.14 | convolution fusion | flops 2685992960 | bytes 11403264 | tf_op jit(solution)/shard_map/dot_general | solution.py:153
  102.1 0.0 all-gather.5.cloned.1.call-update
  102.1 0.2 broadcast_in_dim.59
  102.3 57.7 %all_to_all.52 = bf16[8,256,512]{2,1,0:T(8,128)(2,1)S(1)} all-to-all(bf16[8,256,512]{2,1,0:T(8,128)(2,1)S(1)} %broadcast_in_dim.59), channel_id=1, replica_groups=mesh['group'=8,'dp_0'=2,'dp_1'=4,'dp_2'=2] {'dp_0','dp_1'}, dimensions={0} | all-to-all | bytes 4194304 | tf_op jit(solution)/shard_map/all_to_all | solution.py:19
  160.0 0.5 broadcast_in_dim.60
  160.5 7.1 %all_to_all.53 = bf16[2,8,256,512]{3,2,1,0:T(8,128)(2,1)S(1)} all-to-all(bf16[2,8,256,512]{3,2,1,0:T(8,128)(2,1)S(1)} %broadcast_in_dim.60), channel_id=1, replica_groups=mesh['group'=8,'dp_0'=2,'dp_1'=4,'dp_2'=2] {'dp_2'}, dimensions={0} | all-to-all | bytes 8388608 | tf_op jit(solution)/shard_map/all_to_all | solution.py:19
  167.6 2.5 copy.47
  170.1 12.0 %all-gather.5.cloned.1.call-done = bf16[640,4096]{1,0:T(8,128)(2,1)} async-done(((bf16[640,512]{1,0:T(8,128)(2,1)}), bf16[640,4096]{1,0:T(8,128)(2,1)}) %all-gather.5.cloned.1.call-update) | async-done | bytes 5242896 | tf_op jit(solution)/shard_map/all_gather | solution.py:151
  182.1 6.3 %multiply_convert_fusion = (bf16[640,512]{1,0:T(8,128)(2,1)S(1)}, f32[640,512]{1,0:T(8,128)S(1)}) fusion(bf16[640,4096]{1,0:T(8,128)(2,1)} %all-gather.5.cloned.1.call-done, bf16[4096,512]{1,0:T(8,128)(2,1)} %bitcast.71), kind=kOutput, calls=%fused_computation.13 | convolution fusion | flops 2685992960 | bytes 11403264 | tf_op jit(solution)/shard_map/dot_general | solution.py:153
  188.4 0.3 fusion.20
  188.7 0.8 broadcast_in_dim.61
  189.5 5.8 %all-to-all-start.4 = ((f32[8,640,19]{1,2,0:T(8,128)}), f32[8,640,19]{1,2,0:T(8,128)S(1)}, u32[]{:S(2)}, u32[]{:S(2)}) async-start(f32[8,640,19]{1,2,0:T(8,128)} %broadcast_in_dim.61), calls=%async_computation.4 | async-start | bytes 983040 | tf_op jit(solution)/shard_map/all_to_all | solution.py:19
  195.4 0.0 reduce-scatter.2.cloned.1.call-start
  195.5 9.1 %all-to-all-done.4 = f32[8,640,19]{1,2,0:T(8,128)S(1)} async-done(((f32[8,640,19]{1,2,0:T(8,128)}), f32[8,640,19]{1,2,0:T(8,128)S(1)}, u32[]{:S(2)}, u32[]{:S(2)}) %all-to-all-start.4) | async-done | bytes 389152 | tf_op jit(solution)/shard_map/all_to_all | solution.py:19
  204.7 0.1 reshape.32
  204.9 0.1 slice.56
  205.0 0.1 multiply_bitcast_fusion.1
  205.1 0.1 copy.51
  205.2 0.1 copy.50
  205.3 4.7 %while.17 = (s32[]{:T(128)}, f32[8]{0:T(128)S(1)}, f32[63,8]{1,0:T(8,128)S(1)}, f32[63,8]{1,0:T(8,128)S(1)}, f32[63,8]{1,0:T(8,128)S(1)}, /*index=5*/s32[]{:T(128)}, s32[]{:T(128)}, s32[]{:T(128)}) while((s32[]{:T(128)}, f32[8]{0:T(128)S(1)}, f32[63,8]{1,0:T(8,128)S(1)}, f32[63,8]{1,0:T(8,128)S(1)}, f32[63,8]{1,0:T(8,128)S(1)}, ...), condition=%wide.region_5.7_spmd.clone, body=%wide.region_4.6_spmd.clone.sunk | while | flops 28 | bytes 315 | solution.py:109
  210.0 0.1 copy.52
  210.1 0.1 slice.55
  210.2 0.1 fusion.18
  210.3 0.1 convert_element_type.52
  210.4 0.5 fusion.4
  210.9 1.7 copy-done.2
  212.6 4.6 %convolution_convert_fusion.2 = bf16[512,4096]{1,0:T(8,128)(2,1)} fusion(bf16[512,512]{1,0:T(8,128)(2,1)S(1)} %fusion.4, bf16[4096,512]{1,0:T(8,128)(2,1)S(1)} %bitcast.72), kind=kOutput, calls=%fused_computation.5 | convolution fusion | flops 2149580800 | bytes 8912896 | tf_op jit(solution)/shard_map/dot_general | solution.py:75
  217.3 0.2 copy.56
  217.5 0.1 reshape.33
  217.6 0.4 convolution_bitcast_fusion
  218.0 0.8 reshape.35
  218.8 4.6 %convolution_convert_fusion = bf16[4096,512]{1,0:T(8,128)(2,1)S(1)} fusion(bf16[512,512]{1,0:T(8,128)(2,1)S(1)} %fusion.4, bf16[640,4096]{1,0:T(8,128)(2,1)} %all-gather.5.cloned.1.call-done), kind=kOutput, calls=%fused_computation.3 | convolution fusion | flops 2149580800 | bytes 8912896 | tf_op jit(solution)/shard_map/dot_general | solution.py:69
  223.4 0.4 copy.60
  223.7 8.2 %all_to_all.54 = bf16[2,8,256,512]{3,2,1,0:T(8,128)(2,1)} all-to-all(bf16[2,8,256,512]{3,2,1,0:T(8,128)(2,1)S(1)} %bitcast.70), channel_id=1, replica_groups=mesh['group'=8,'dp_0'=2,'dp_1'=4,'dp_2'=2] {'dp_2'}, dimensions={0} | all-to-all | bytes 8388608 | tf_op jit(solution)/shard_map/all_to_all | solution.py:54
  231.9 7.2 %all-to-all-start.9 = ((f32[16,1,608]{2,1,0:T(1,128)}), f32[16,1,608]{2,1,0:T(1,128)S(1)}, u32[]{:S(2)}, u32[]{:S(2)}) async-start(f32[16,1,608]{2,1,0:T(1,128)} %reshape.35), calls=%async_computation.10 | async-start | bytes 81920 | tf_op jit(solution)/shard_map/all_to_all | solution.py:48
  239.1 5.0 %reduce_sum.92 = bf16[8,256,512]{2,1,0:T(8,128)(2,1)} reduce(bf16[2,8,256,512]{3,2,1,0:T(8,128)(2,1)} %all_to_all.54, bf16[]{:T(256)} %constant.71.clone.1), dimensions={0}, to_apply=%region_10.12 | reduce | flops 1048576 | bytes 6291458 | tf_op jit(solution)/shard_map/reduce_sum | solution.py:55
  244.1 26.5 %reduce-scatter.2.cloned.1.call-done = bf16[512,512]{1,0:T(8,128)(2,1)} async-done(((bf16[512,4096]{1,0:T(8,128)(2,1)}), bf16[512,512]{1,0:T(8,128)(2,1)}) %reduce-scatter.2.cloned.1.call-update) | async-done | bytes 524304 | tf_op jit(solution)/shard_map/reduce_scatter | solution.py:196
  270.6 4.9 %convolution_convert_fusion.1 = bf16[4096,512]{1,0:T(8,128)(2,1)S(1)} fusion(bf16[640,4096]{1,0:T(8,128)(2,1)} %all-gather.3.cloned.1.call-done, f32[640,512]{1,0:T(8,128)S(1)} %copy-done.7, bf16[512,512]{1,0:T(8,128)(2,1)} %reduce-scatter.2.cloned.1.call-done), kind=kOutput, calls=%fused_computation.4 | convolution fusion | flops 2152202240 | bytes 9961472 | tf_op jit(solution)/shard_map/dot_general | solution.py:69
  275.5 2.4 copy.61
  277.9 11.9 %all_to_all.55 = bf16[2,8,256,512]{3,2,1,0:T(8,128)(2,1)} all-to-all(bf16[2,8,256,512]{3,2,1,0:T(8,128)(2,1)} %bitcast.69), channel_id=1, replica_groups=mesh['group'=8,'dp_0'=2,'dp_1'=4,'dp_2'=2] {'dp_2'}, dimensions={0} | all-to-all | bytes 8388608 | tf_op jit(solution)/shard_map/all_to_all | solution.py:54
  289.7 6.5 %all-to-all-start.8 = ((bf16[8,256,512]{2,1,0:T(8,128)(2,1)}), bf16[8,256,512]{2,1,0:T(8,128)(2,1)S(1)}, u32[]{:S(2)}, u32[]{:S(2)}) async-start(bf16[8,256,512]{2,1,0:T(8,128)(2,1)} %reduce_sum.92), calls=%async_computation.9 | async-start | bytes 4194304 | tf_op jit(solution)/shard_map/all_to_all | solution.py:62
  296.3 4.9 %reduce_sum.90 = bf16[8,256,512]{2,1,0:T(8,128)(2,1)} reduce(bf16[2,8,256,512]{3,2,1,0:T(8,128)(2,1)} %all_to_all.55, bf16[]{:T(256)} %constant.71.clone.1), dimensions={0}, to_apply=%region_8.10 | reduce | flops 1048576 | bytes 6291458 | tf_op jit(solution)/shard_map/reduce_sum | solution.py:55
  301.2 21.8 %all-to-all-done.8 = bf16[8,256,512]{2,1,0:T(8,128)(2,1)S(1)} async-done(((bf16[8,256,512]{2,1,0:T(8,128)(2,1)}), bf16[8,256,512]{2,1,0:T(8,128)(2,1)S(1)}, u32[]{:S(2)}, u32[]{:S(2)}) %all-to-all-start.8) | async-done | bytes 2097184 | tf_op jit(solution)/shard_map/all_to_all | solution.py:62
  323.0 4.8 %all-to-all-start.6 = ((bf16[8,256,512]{2,1,0:T(8,128)(2,1)}), bf16[8,256,512]{2,1,0:T(8,128)(2,1)}, u32[]{:S(2)}, u32[]{:S(2)}) async-start(bf16[8,256,512]{2,1,0:T(8,128)(2,1)} %reduce_sum.90), calls=%async_computation.7 | async-start | bytes 4194304 | tf_op jit(solution)/shard_map/all_to_all | solution.py:62
  327.8 0.6 slice.70
  328.4 0.5 broadcast.57
  328.9 0.7 reduce.2
  329.6 0.1 reshape.36
  329.7 0.6 bitcast_reduce_fusion
  330.3 0.3 convert_reduce_fusion
  330.6 23.8 %all-to-all-done.6 = bf16[8,256,512]{2,1,0:T(8,128)(2,1)} async-done(((bf16[8,256,512]{2,1,0:T(8,128)(2,1)}), bf16[8,256,512]{2,1,0:T(8,128)(2,1)}, u32[]{:S(2)}, u32[]{:S(2)}) %all-to-all-start.6) | async-done | bytes 2097184 | tf_op jit(solution)/shard_map/all_to_all | solution.py:62
  354.4 1.9 convert_reduce_fusion.1
  356.4 1.1 pad_maximum_fusion
  (160 shorter events, 4.1 us)
Async XLA Ops:
  7.2 181.2 %copy-start = (bf16[512,19]{0,1:T(8,128)(2,1)S(1)}, bf16[512,19]{0,1:T(8,128)(2,1)}, u32[]{:S(2)}) copy-start(bf16[512,19]{0,1:T(8,128)(2,1)} %param.14) | copy-start | bytes 58372
  7.2 86.9 %all-gather.3.cloned.1.call-start = ((), (), s32[]{:S(2)}) async-start(), calls=%async_computation.11 | async-start | bytes 5898240 | tf_op jit(solution)/shard_map/all_gather | solution.py:151
  9.2 172.9 %all-gather.5.cloned.1.call-start = ((), (), s32[]{:S(2)}) async-start(), calls=%async_computation.12 | async-start | bytes 5898240 | tf_op jit(solution)/shard_map/all_gather | solution.py:151
  182.1 13.3 %copy-start.3 = (f32[8,63,18]{1,0,2:T(8,128)S(1)}, f32[8,63,18]{1,0,2:T(8,128)}, u32[]{:S(2)}) copy-start(f32[8,63,18]{1,0,2:T(8,128)} %param.15) | copy-start | bytes 108868
  182.1 22.7 %copy-start.6 = (s32[8,63]{1,0:T(8,128)S(1)}, s32[8,63]{1,0:T(8,128)}, u32[]{:S(2)}) copy-start(s32[8,63]{1,0:T(8,128)} %param.16) | copy-start | bytes 6052
  182.1 22.9 %copy-start.4 = (s32[8,63]{1,0:T(8,128)S(1)}, s32[8,63]{1,0:T(8,128)}, u32[]{:S(2)}) copy-start(s32[8,63]{1,0:T(8,128)} %param.18) | copy-start | bytes 6052
  182.1 22.9 %copy-start.5 = (f32[8,63]{1,0:T(8,128)S(1)}, f32[8,63]{1,0:T(8,128)}, u32[]{:S(2)}) copy-start(f32[8,63]{1,0:T(8,128)} %param.17) | copy-start | bytes 6052
  189.5 15.1 %all-to-all-start.4 = ((f32[8,640,19]{1,2,0:T(8,128)}), f32[8,640,19]{1,2,0:T(8,128)S(1)}, u32[]{:S(2)}, u32[]{:S(2)}) async-start(f32[8,640,19]{1,2,0:T(8,128)} %broadcast_in_dim.61), calls=%async_computation.4 | async-start | bytes 983040 | tf_op jit(solution)/shard_map/all_to_all | solution.py:19
  195.4 75.2 %reduce-scatter.2.cloned.1.call-start = ((), (), s32[]{:S(2)}) async-start(), calls=%async_computation.13 | async-start | bytes 4718592 | tf_op jit(solution)/shard_map/reduce_scatter | solution.py:196
  210.4 2.2 copy-start.2
  231.9 38.7 %copy-start.7 = (f32[640,512]{1,0:T(8,128)S(1)}, f32[640,512]{1,0:T(8,128)}, u32[]{:S(2)}) copy-start(f32[640,512]{1,0:T(8,128)} %get-tuple-element.155) | copy-start | bytes 3932164
  231.9 46.0 %all-to-all-start.9 = ((f32[16,1,608]{2,1,0:T(1,128)}), f32[16,1,608]{2,1,0:T(1,128)S(1)}, u32[]{:S(2)}, u32[]{:S(2)}) async-start(f32[16,1,608]{2,1,0:T(1,128)} %reshape.35), calls=%async_computation.10 | async-start | bytes 81920 | tf_op jit(solution)/shard_map/all_to_all | solution.py:48
  289.7 33.3 %all-to-all-start.8 = ((bf16[8,256,512]{2,1,0:T(8,128)(2,1)}), bf16[8,256,512]{2,1,0:T(8,128)(2,1)S(1)}, u32[]{:S(2)}, u32[]{:S(2)}) async-start(bf16[8,256,512]{2,1,0:T(8,128)(2,1)} %reduce_sum.92), calls=%async_computation.9 | async-start | bytes 4194304 | tf_op jit(solution)/shard_map/all_to_all | solution.py:62
  323.0 31.5 %all-to-all-start.6 = ((bf16[8,256,512]{2,1,0:T(8,128)(2,1)}), bf16[8,256,512]{2,1,0:T(8,128)(2,1)}, u32[]{:S(2)}, u32[]{:S(2)}) async-start(bf16[8,256,512]{2,1,0:T(8,128)(2,1)} %reduce_sum.90), calls=%async_computation.7 | async-start | bytes 4194304 | tf_op jit(solution)/shard_map/all_to_all | solution.py:62
  327.7 29.7 %copy-start.1 = (bf16[512,19]{0,1:T(8,128)(2,1)S(1)}, bf16[512,19]{0,1:T(8,128)(2,1)}, u32[]{:S(2)}) copy-start(bf16[512,19]{0,1:T(8,128)(2,1)} %param.14) | copy-start | bytes 58372
Sparse Core Ops, SparseCore 0:
  10.2 83.8 all-gather.2
  102.2 79.8 all-gather.4
  217.3 53.2 reduce-scatter.1
where the time goes:
time: 365 us; the launch traced here: 364 us
  blocking collectives  148 us (41%)
  waiting for transfers between devices  111 us (30%)
  matrix products  29.5 us (8%)
  starting transfers between devices  24.5 us (7%)
  other arithmetic  18.2 us (5%)
  local copies, waits for them, and re-layouts  18 us (5%)
  between operations  14 us (4%)
    all_to_all x4, blocking collectives, from_everyone(): lax.all_to_all(jnp.broadcast_to(array[None], (size, *array.shape)), axis,...  128 us
    all_to_all x2, waiting for transfers between devices, sum_in_two_steps(): lax.all_to_all(nearer.astype(jnp.bfloat16), far, split_axis=0, concat_axi...  45.6 us
    all_gather x2, waiting for transfers between devices, per_device(): forward_whole = lax.all_gather(current, 'group', axis=1, tiled=True)  29.5 us
    reduce_scatter x1, waiting for transfers between devices, per_device(): lax.psum_scatter(full_grad.astype(jnp.bfloat16), 'group', scatter_dimensi...  26.5 us
    all_to_all x2, blocking collectives, sent_and_summed(): lax.all_to_all(parts, axis, split_axis=0, concat_axis=0, tiled=True)  20 us
    dot_general x2, matrix products, per_device(): jnp.dot(forward_whole, gathered_weights[forward_layer_index], preferred_e...  14.3 us
    all_to_all x2, starting transfers between devices, sum_in_two_steps(): lax.all_to_all(nearer.astype(jnp.bfloat16), far, split_axis=0, concat_axi...  11.3 us
    reduce_sum x2, other arithmetic, sent_and_summed(): return arrived.astype(jnp.float32).sum(axis=0)  9.95 us
  transfers between devices with their start and end apart: 7, of which 6 were waited for; matrix products, arithmetic and copies ran while one was open for 9% of the time, Pallas kernels for 0%

commit v1 on v0

v1 whole, which is shorter than its diff:
```python
import functools

import jax
import jax.numpy as jnp
from jax import lax
from jax.experimental import pallas as pl
from jax.experimental.pallas import tpu as pltpu
from jax.sharding import Mesh
from jax.sharding import PartitionSpec as P

AXES = ("xl", "y", "xh", "z", "c")
SIZES = (2, 4, 2, 4, 2)
DP = ("xh", "z", "c")
GROUP = ("xl", "y")
MESH = pl.DeviceIdType.MESH
F32 = jnp.float32
BF16 = jnp.bfloat16

discount_rate = 0.99
value_weight = 0.5
entropy_weight = 0.1
loss_divisor = 16.0

TR = 512
AR = 128
FB = 512
WB = 256
STEPS = 64
ACT = 18
ER = 272
N_SEM = 192


def nn(a, b):
    return jnp.dot(a, b, preferred_element_type=F32)


def nt(a, b):
    return lax.dot_general(a, b, (((1,), (1,)), ((), ())), preferred_element_type=F32)


def tn(a, b):
    return lax.dot_general(a, b, (((0,), (0,)), ((), ())), preferred_element_type=F32)


def vtrace(logits, behave, action, reward, finished):
    row = lax.broadcasted_iota(jnp.int32, logits.shape, 0)
    step = lax.broadcasted_iota(jnp.int32, reward.shape, 1)
    live = step < STEPS - 1
    is_act = row < ACT

    def log_softmax(values):
        top = jnp.max(jnp.where(is_act, values, -3.0e38), axis=0, keepdims=True)
        shifted = jnp.where(is_act, values - top, 0.0)
        total = jnp.sum(jnp.where(is_act, jnp.exp(shifted), 0.0), axis=0, keepdims=True)
        return jnp.where(is_act, shifted - jnp.log(total), 0.0)

    log_policy = log_softmax(logits)
    log_behave = log_softmax(behave)
    chosen = jnp.where(row.astype(F32) == action, 1.0, 0.0)
    ratio = jnp.exp(jnp.sum((log_policy - log_behave) * chosen, axis=0, keepdims=True))
    clipped = jnp.minimum(ratio, 1.0)
    discount = discount_rate * (1.0 - finished)
    current = logits[ACT : ACT + 1, :]
    following = pltpu.roll(current, 127, 1)
    delta = jnp.where(live, clipped * (reward + discount * following - current), 0.0)
    factor = jnp.where(live, discount * clipped, 0.0)
    for shift in (1, 2, 4, 8, 16, 32):
        delta = delta + factor * pltpu.roll(delta, 128 - shift, 1)
        factor = factor * pltpu.roll(factor, 128 - shift, 1)
    targets = current + delta
    next_targets = pltpu.roll(targets, 127, 1)
    advantage = clipped * (reward + discount * next_targets - current)
    probability = jnp.where(is_act, jnp.exp(log_policy), 0.0)
    entropy = -jnp.sum(probability * log_policy, axis=0, keepdims=True)
    logit_grad = (
        -advantage * (chosen - probability)
        + entropy_weight * probability * (log_policy + entropy)
    ) / loss_divisor
    value_grad = -value_weight * (targets - current) / loss_divisor
    grad = jnp.where(is_act, logit_grad, jnp.where(row == ACT, value_grad, 0.0))
    return jnp.where(live, grad, 0.0)


def kernel(
    obs, nxt, wts, head, acting, actions, rewards, finished,
    dw_out, hg_out, al_out,
    xf0, xf1, wf0, wf1, acc, slope0, slope1, x2, headt, tmp, misc,
    hs, hr, ha_s, ha_r, og_s, og_r, pg1, pg0, hgp,
    sb, rb, own,
    dws1, dwr1, q1, rz1a, rz2a, xs1, rx1,
    dws0, dwr0, q0, rz1b, rz2b, xs0, rx0,
    ssem, rsem, lsem,
):
    xl, y, xh, z, c = (lax.axis_index(a) for a in AXES)
    g = xl * 4 + y
    xf, wf = (xf0, xf1), (wf0, wf1)

    def rel_g(dx, dy):
        return ((xl + dx) % 2) * 4 + (y + dy) % 4

    def rel_w(dx, dz):
        return ((xh + dx) % 2) * 4 + (z + dz) % 4

    x_peer = {"xl": 1 - xl}
    y_up, y_down = {"y": (y + 1) % 4}, {"y": (y + 3) % 4}
    h_peer = {"xh": 1 - xh}
    z_up, z_down = {"z": (z + 1) % 4}, {"z": (z + 3) % 4}
    sibling = {"c": 1 - c}

    count = [0]
    sent = []

    def send(src, dst, device):
        index = count[0]
        count[0] += 1
        copy = pltpu.make_async_remote_copy(
            src_ref=src, dst_ref=dst, send_sem=ssem.at[index], recv_sem=rsem.at[index],
            device_id=device, device_id_type=MESH,
        )
        copy.start()
        sent.append(copy)
        return copy

    cb = pl.multiple_of(c * WB, WB)
    wg = xh * 4 + z
    loads = [
        pltpu.make_async_copy(obs, xf0.at[g, pl.ds(0, TR), :], lsem.at[0]),
        pltpu.make_async_copy(wts.at[0], wf0.at[wg, pl.ds(cb, WB), :], lsem.at[1]),
        pltpu.make_async_copy(wts.at[1], wf1.at[wg, pl.ds(cb, WB), :], lsem.at[2]),
        pltpu.make_async_copy(nxt, xf0.at[g, pl.ds(TR, AR), :], lsem.at[3]),
    ]
    for load in loads:
        load.start()

    barrier = pltpu.get_barrier_semaphore()
    friends = [h_peer, z_up, z_down, sibling]
    for k in range(1, 8):
        gt = (g + k) % 8
        friends.append({"xl": gt // 4, "y": gt % 4})
    for friend in friends:
        pl.semaphore_signal(barrier, inc=1, device_id=friend, device_id_type=MESH)
    pl.semaphore_wait(barrier, len(friends))

    def x_start(layer, first, amount):
        buf, half = xf[layer], amount // 2
        lo, hi = pl.ds(first, half), pl.ds(first + half, half)

        def go(block, rows, device):
            return send(buf.at[block, rows, :], buf.at[block, rows, :], device)

        st = {"go": go, "lo": lo, "hi": hi}
        return st

    def x_own(st, rows):
        go, lo = st["go"], st["lo"]
        if rows == "lo":
            st["up_lo"] = go(g, lo, y_up)
            st["x_lo"] = go(g, lo, x_peer)
            st["dn_lo"] = None
        else:
            st["dn_hi"] = go(g, st["hi"], y_down)
            st["x_hi"] = go(g, st["hi"], x_peer)
            st["up_hi"] = go(g, st["hi"], y_up)
            st["dn_lo"] = go(g, lo, y_down)

    def x_fwd1(st):
        go = st["go"]
        st["up_lo"].wait_recv()
        st["f_lo"] = go(rel_g(0, 3), st["lo"], y_up)
        st["dn_hi"].wait_recv()
        st["f_hi"] = go(rel_g(0, 1), st["hi"], y_down)

    def x_fwd2(st):
        go, far = st["go"], rel_g(1, 0)
        st["x_lo"].wait_recv()
        st["p_up_lo"] = go(far, st["lo"], y_up)
        st["p_dn_lo"] = go(far, st["lo"], y_down)
        st["x_hi"].wait_recv()
        st["p_up_hi"] = go(far, st["hi"], y_up)
        st["p_dn_hi"] = go(far, st["hi"], y_down)

    def x_fwd3(st):
        go, far = st["go"], rel_g(0, 2)
        st["f_lo"].wait_recv()
        st["x2_lo"] = go(far, st["lo"], x_peer)
        st["f_hi"].wait_recv()
        st["x2_hi"] = go(far, st["hi"], x_peer)

    def x_near(st):
        st["up_hi"].wait_recv()
        st["dn_lo"].wait_recv()

    def x_far(st):
        for name in ("p_up_lo", "p_up_hi", "p_dn_lo", "p_dn_hi", "x2_lo", "x2_hi"):
            st[name].wait_recv()

    half_w = WB // 2

    def w_piece(block, part):
        if part == "all":
            return (block, pl.ds(cb, WB), slice(None))
        start = cb if part == "lo" else cb + half_w
        return (block, pl.ds(pl.multiple_of(start, half_w), half_w), slice(None))

    def w_start(layer):
        buf = wf[layer]

        def go(block, part, device):
            where = w_piece(block, part)
            return send(buf.at[where], buf.at[where], device)

        st = {"go": go}
        st["up_lo"] = go(wg, "lo", z_up)
        st["dn_hi"] = go(wg, "hi", z_down)
        st["h"] = go(wg, "all", h_peer)
        st["up_hi"] = go(wg, "hi", z_up)
        st["dn_lo"] = go(wg, "lo", z_down)
        st["sib"] = [go(wg, "all", sibling)]
        return st

    def w_share(st, block):
        st["sib"].append(st["go"](block, "all", sibling))

    def w_fwd1(st):
        go = st["go"]
        st["up_lo"].wait_recv()
        st["f_lo"] = go(rel_w(0, 3), "lo", z_up)
        st["dn_hi"].wait_recv()
        st["f_hi"] = go(rel_w(0, 1), "hi", z_down)

    def w_fwd2(st):
        go, far = st["go"], rel_w(1, 0)
        st["h"].wait_recv()
        st["h_up_lo"] = go(far, "lo", z_up)
        st["h_dn_hi"] = go(far, "hi", z_down)
        st["h_up_hi"] = go(far, "hi", z_up)
        st["h_dn_lo"] = go(far, "lo", z_down)
        w_share(st, far)
        st["up_hi"].wait_recv()
        w_share(st, rel_w(0, 3))
        st["dn_lo"].wait_recv()
        w_share(st, rel_w(0, 1))

    def w_fwd3(st):
        go = st["go"]
        st["h_up_lo"].wait_recv()
        st["g_lo"] = go(rel_w(1, 3), "lo", z_up)
        st["h_dn_hi"].wait_recv()
        st["g_hi"] = go(rel_w(1, 1), "hi", z_down)
        st["f_lo"].wait_recv()
        st["f_hi"].wait_recv()
        w_share(st, rel_w(0, 2))

    def w_finish(st):
        st["h_up_hi"].wait_recv()
        w_share(st, rel_w(1, 3))
        st["h_dn_lo"].wait_recv()
        w_share(st, rel_w(1, 1))
        st["g_lo"].wait_recv()
        st["g_hi"].wait_recv()
        w_share(st, rel_w(1, 2))
        for copy in st["sib"]:
            copy.wait_recv()

    def blocks(layer, first, amount, j0, j1, fresh):
        buf, weights = xf[layer], wf[layer]
        tile = min(amount, 256)
        if fresh:
            for r in range(0, amount, tile):
                acc[first + r : first + r + tile, :] = nn(buf[g, first + r : first + r + tile, :], weights[g])

        def body(j, carry):
            block = ((xl + j // 4) % 2) * 4 + (y + j % 4) % 4
            for r in range(0, amount, tile):
                rows = slice(first + r, first + r + tile)
                acc[rows, :] += nn(buf[block, rows, :], weights[block])
            return carry

        lax.fori_loop(j0, j1, body, 0)

    def activate(first, amount, out, slope, tile=64):
        def body(i, carry):
            rows = pl.ds(pl.multiple_of(first + i * tile, tile), tile)
            value = acc[rows, :]
            sigma = jax.nn.sigmoid(value)
            out(rows, (value * sigma).astype(BF16))
            if slope is not None:
                slope[rows, :] = sigma * (1.0 + value * (1.0 - sigma))
            return carry

        lax.fori_loop(0, amount // tile, body, 0)

    def into_x1(rows, value):
        xf1[g, rows, :] = value

    def into_x2(rows, value):
        x2[rows, :] = value

    loads[0].wait()
    loads[1].wait()
    w0 = w_start(0)
    t0 = x_start(0, 0, TR)
    x_own(t0, "lo")
    x_own(t0, "hi")
    loads[2].wait()
    loads[3].wait()

    tmp[...] = jnp.zeros_like(tmp)
    tmp[:, 0 : ACT + 1] = head[...].astype(F32)
    headt[...] = tmp[...].T.astype(BF16)
    tmp[0:128, :] = jnp.zeros((128, 128), F32)
    tmp[0 : STEPS - 1, 0:ACT] = acting[g]
    misc[...] = jnp.zeros_like(misc)
    misc[0:24, :] = tmp[0:128, :].T[0:24, :]
    misc[24:25, 0 : STEPS - 1] = actions[pl.ds(g, 1), :].astype(F32)
    misc[25:26, 0 : STEPS - 1] = rewards[pl.ds(g, 1), :]
    misc[26:27, 0 : STEPS - 1] = finished[pl.ds(g, 1), :].astype(F32)
    hs[...] = jnp.zeros_like(hs)
    tmp[0:128, :] = jnp.zeros((128, 128), F32)

    w_fwd1(w0)
    x_fwd1(t0)
    x_fwd2(t0)
    w_fwd2(w0)
    w_fwd3(w0)
    x_fwd3(t0)
    w_finish(w0)
    w1 = w_start(1)
    x_near(t0)
    blocks(0, 0, TR, 1, 5, True)
    w_fwd1(w1)
    x_far(t0)
    blocks(0, 0, TR, 5, 8, False)

    t1 = x_start(1, 0, TR)
    activate(0, TR // 2, into_x1, slope0)
    x_own(t1, "lo")
    activate(TR // 2, TR // 2, into_x1, slope0)
    x_own(t1, "hi")

    w_fwd2(w1)
    x_fwd1(t1)
    x_fwd2(t1)
    w_fwd3(w1)
    x_fwd3(t1)
    a0 = x_start(0, TR, AR)
    x_own(a0, "lo")
    x_own(a0, "hi")
    w_finish(w1)
    x_near(t1)
    blocks(1, 0, TR, 1, 5, True)
    x_far(t1)
    blocks(1, 0, TR, 5, 8, False)
    activate(0, TR, into_x2, slope1)

    part = nt(headt[0:32, :], x2[0:TR, :])
    for r in range(8):
        hs[r, :, 0:STEPS] = part[0:24, STEPS * r : STEPS * (r + 1)]
    heads = []
    for k in range(1, 8):
        gt = (g + k) % 8
        heads.append(send(hs.at[gt], hr.at[g], {"xl": gt // 4, "y": gt % 4}))
    x_fwd1(a0)
    x_fwd2(a0)
    x_fwd3(a0)
    total = hs[g]
    for k in range(1, 8):
        heads[k - 1].wait_recv()
    for k in range(1, 8):
        total = total + hr[(g + 8 - k) % 8]
    grad = vtrace(total, misc[0:24, :], misc[24:25, :], misc[25:26, :], misc[26:27, :])
    tmp[0:24, :] = grad
    og_s[...] = tmp[0:128, :].T[0:STEPS, :].astype(BF16)
    og_r[g] = og_s[...]
    outs = []
    for k in range(1, 8):
        gt = (g + k) % 8
        outs.append(send(og_s, og_r.at[g], {"xl": gt // 4, "y": gt % 4}))
    for copy in outs:
        copy.wait_recv()

    def slopes(first, amount):
        for r in range(first, first + amount, 256):
            rows = slice(r, r + 256)
            og = og_r[r // STEPS : (r + 256) // STEPS].reshape(256, 128)
            pg1[rows, :] = (nn(og, headt[...]) * slope1[rows, :]).astype(BF16)

    slopes(0, TR)
    lo, hi = slice(0, TR // 2), slice(TR // 2, TR)

    def piece(block, rows):
        return nt(pg1[rows, :], wf1[block])

    def push(k, rows, device):
        start = 0 if rows is lo else TR // 2
        where = (k, pl.ds(start, TR // 2), slice(None))
        return send(sb.at[where], rb.at[where], device)

    where_g = (rel_g(1, 2), rel_g(1, 1), rel_g(1, 3), rel_g(0, 1), rel_g(0, 3), rel_g(0, 2), rel_g(1, 0))

    def make(k):
        for rows in (lo, hi):
            sb[k, rows, :] = piece(where_g[k], rows).astype(BF16)

    make(0)
    s1 = [push(0, lo, x_peer), push(0, hi, x_peer)]
    make(1)
    s2u = [push(1, lo, y_up), push(1, hi, y_up)]
    make(2)
    s2d = [push(2, lo, y_down), push(2, hi, y_down)]
    make(3)
    s5u = [push(3, hi, y_up)]
    make(4)
    s5d = [push(4, lo, y_down)]

    def head_rows(dst, i, block, core):
        base = pl.multiple_of((2 * block + core) * 32, 32)
        dst[i, WB:ER, 0:128] = hgp[pl.ds(base, 16), :].astype(BF16)
        dst[i, WB:ER, 128:256] = hgp[pl.ds(pl.multiple_of(base + 16, 16), 16), :].astype(BF16)
        dst[i, WB:ER, 256:512] = jnp.zeros((ER - WB, 256), BF16)

    def dw_block(i):
        return ((xh + 1 - i % 2) % 2) * 4 + (z + 2 + i // 2) % 4

    def dw_open(layer, pg, dws, dwr, extra):
        base = count[0]
        count[0] += 8
        other = pl.multiple_of((1 - c) * WB, WB)

        def copy_of(i):
            return pltpu.make_async_remote_copy(
                src_ref=dws.at[i], dst_ref=dwr.at[i], send_sem=ssem.at[base + i], recv_sem=rsem.at[base + i],
                device_id=sibling, device_id_type=MESH,
            )

        def body(i, carry):
            block = dw_block(i)
            term = tn(xf[layer][block, 0:TR, pl.ds(other, WB)], pg[...])
            dws[i, 0:WB, :] = term.astype(BF16)
            if extra:
                head_rows(dws, i, block, 1 - c)
            copy_of(i).start()
            return carry

        lax.fori_loop(0, 8, body, 0)
        return copy_of

    def dw_close(layer, pg, copy_of, dwr, q, extra):
        def body(i, carry):
            block = dw_block(i)
            term = tn(xf[layer][block, 0:TR, pl.ds(cb, WB)], pg[...])
            copy_of(i).wait_recv()
            q[i, 0:WB, :] = (term + dwr[i, 0:WB, :].astype(F32)).astype(BF16)
            if extra:
                head_rows(q, i, block, c)
                q[i, WB:ER, :] = (q[i, WB:ER, :].astype(F32) + dwr[i, WB:ER, :].astype(F32)).astype(BF16)
            return carry

        lax.fori_loop(0, 8, body, 0)

    def z_first(q, rz1, size):
        low, high = pl.ds(0, 128), pl.ds(128, size - 128)
        st = {}
        for xr in (0, 1):
            st["a", xr] = send(q.at[xr, low, :], rz1.at[xr, low, :], z_up)
            st["b", xr] = send(q.at[xr, high, :], rz1.at[xr, high, :], z_down)
        return st

    def z_plain(st, q, rz2, size):
        low, high = pl.ds(0, 128), pl.ds(128, size - 128)
        for xr in (0, 1):
            st["up_hi", xr] = send(q.at[6 + xr, high, :], rz2.at[xr, 0, high, :], z_up)
            st["dn_lo", xr] = send(q.at[2 + xr, low, :], rz2.at[xr, 1, low, :], z_down)

    def z_added(st, q, rz1, rz2, size):
        low, high = pl.ds(0, 128), pl.ds(128, size - 128)
        for xr in (0, 1):
            st["a", xr].wait_recv()
            q[6 + xr, 0:128, :] = (q[6 + xr, 0:128, :].astype(F32) + rz1[xr, 0:128, :].astype(F32)).astype(BF16)
            st["up_lo", xr] = send(q.at[6 + xr, low, :], rz2.at[xr, 0, low, :], z_up)
            st["b", xr].wait_recv()
            q[2 + xr, 128:size, :] = (
                q[2 + xr, 128:size, :].astype(F32) + rz1[xr, 128:size, :].astype(F32)
            ).astype(BF16)
            st["dn_hi", xr] = send(q.at[2 + xr, high, :], rz2.at[xr, 1, high, :], z_down)

    def z_sum(st, xr, q, rz2):
        for name in ("up_hi", "dn_lo", "up_lo", "dn_hi"):
            st[name, xr].wait_recv()
        return q[4 + xr].astype(F32) + rz2[xr, 0].astype(F32) + rz2[xr, 1].astype(F32)

    hgp[...] = tn(x2[0:TR, :], og_r[...].reshape(TR, 128))
    copy1 = dw_open(1, pg1, dws1, dwr1, True)
    make(5)
    make(6)
    dw_close(1, pg1, copy1, dwr1, q1, True)
    st1 = z_first(q1, rz1a, ER)
    z_plain(st1, q1, rz2a, ER)
    for rows in (lo, hi):
        own[rows, :] = piece(g, rows)

    def add_in(k, rows, *terms):
        value = sb[k, rows, :].astype(F32)
        for term in terms:
            value = value + rb[term, rows, :].astype(F32)
        sb[k, rows, :] = value.astype(BF16)

    s1[0].wait_recv()
    add_in(5, lo, 0)
    s4u = push(5, lo, y_up)
    s1[1].wait_recv()
    add_in(5, hi, 0)
    s4d = push(5, hi, y_down)
    z_added(st1, q1, rz1a, rz2a, ER)
    s3 = []
    for i, rows in enumerate((lo, hi)):
        s2u[i].wait_recv()
        s2d[i].wait_recv()
        add_in(6, rows, 1, 2)
        s3.append(push(6, rows, x_peer))
    s4u.wait_recv()
    add_in(3, lo, 5)
    s5u.append(push(3, lo, y_up))
    s4d.wait_recv()
    add_in(4, hi, 5)
    s5d.append(push(4, hi, y_down))

    x_near(a0)
    x_far(a0)
    blocks(0, TR, AR, 1, 8, True)
    activate(TR, AR, into_x1, None)

    xs1[...] = z_sum(st1, 0, q1, rz2a).astype(BF16)
    h1 = send(xs1, rx1, h_peer)

    for copy in s5u + s5d + s3:
        copy.wait_recv()
    for r in range(0, TR, 64):
        rows = slice(r, r + 64)
        value = own[rows, :] + rb[3, rows, :].astype(F32) + rb[4, rows, :].astype(F32) + rb[6, rows, :].astype(F32)
        pg0[rows, :] = (value * slope0[rows, :]).astype(BF16)

    a1 = x_start(1, TR, AR)
    x_own(a1, "lo")
    x_own(a1, "hi")
    copy0 = dw_open(0, pg0, dws0, dwr0, False)
    dw_close(0, pg0, copy0, dwr0, q0, False)
    st0 = z_first(q0, rz1b, WB)
    z_plain(st0, q0, rz2b, WB)

    x_fwd1(a1)
    x_fwd2(a1)
    value = z_sum(st1, 1, q1, rz2a)
    h1.wait_recv()
    value = value + rx1[...].astype(F32)
    dw_out[1] = value[0:WB, :]
    hg_out[0:16, :] = value[WB:ER, 0 : ACT + 1]
    hg_out[16:32, :] = value[WB:ER, 128 : 128 + ACT + 1]
    z_added(st0, q0, rz1b, rz2b, WB)
    x_fwd3(a1)
    x_near(a1)
    x_far(a1)
    blocks(1, TR, AR, 1, 8, True)
    activate(TR, AR, into_x2, None)
    ha_s[...] = nt(headt[0:32, :], x2[TR : TR + AR, :])[0:24, :]
    acts = []
    for k in range(1, 8):
        gt = (g + k) % 8
        acts.append(send(ha_s, ha_r.at[g], {"xl": gt // 4, "y": gt % 4}))

    xs0[...] = z_sum(st0, 0, q0, rz2b).astype(BF16)
    h0 = send(xs0, rx0, h_peer)
    for copy in acts:
        copy.wait_recv()
    total = ha_s[...]
    for k in range(1, 8):
        total = total + ha_r[(g + 8 - k) % 8]
    tmp[0:24, :] = total
    al_out[...] = tmp[0:128, :].T[:, 0:ACT]
    value = z_sum(st0, 1, q0, rz2b)
    h0.wait_recv()
    dw_out[0] = value + rx0[...].astype(F32)

    for copy in sent:
        copy.wait_send()

    def drain(i, carry):
        copy1(i).wait_send()
        copy0(i).wait_send()
        return carry

    lax.fori_loop(0, 8, drain, 0)


def per_device(observations, next_observations, trunk_weights, head_weights, acting, actions, rewards, finished):
    v = pltpu.VMEM
    dw_bufs = lambda rows: [
        v((8, rows, FB), BF16), v((8, rows, FB), BF16), v((8, rows, FB), BF16), v((2, rows, FB), BF16),
        v((2, 2, rows, FB), BF16), v((rows, FB), BF16), v((rows, FB), BF16),
    ]
    scratch = [
        v((8, TR + AR, FB), BF16), v((8, TR + AR, FB), BF16), v((8, FB, FB), BF16), v((8, FB, FB), BF16),
        v((TR + AR, FB), F32), v((TR, FB), F32), v((TR, FB), F32), v((TR + AR, FB), BF16),
        v((128, FB), BF16), v((FB, 128), F32), v((32, 128), F32),
        v((8, 24, 128), F32), v((8, 24, 128), F32), v((24, 128), F32), v((8, 24, 128), F32),
        v((STEPS, 128), BF16), v((8, STEPS, 128), BF16), v((TR, FB), BF16), v((TR, FB), BF16), v((FB, 128), F32),
        v((7, TR, FB), BF16), v((7, TR, FB), BF16), v((TR, FB), F32),
        *dw_bufs(ER), *dw_bufs(WB),
        pltpu.SemaphoreType.DMA((N_SEM,)), pltpu.SemaphoreType.DMA((N_SEM,)), pltpu.SemaphoreType.DMA((4,)),
    ]
    hbm = pl.BlockSpec(memory_space=pltpu.HBM)
    vmem = pl.BlockSpec(memory_space=pltpu.VMEM)
    return pl.pallas_call(
        kernel,
        out_shape=(
            jax.ShapeDtypeStruct((2, WB, FB), F32),
            jax.ShapeDtypeStruct((32, ACT + 1), F32),
            jax.ShapeDtypeStruct((AR, ACT), F32),
        ),
        in_specs=[hbm, hbm, hbm, vmem, vmem, vmem, vmem, vmem],
        out_specs=(vmem, vmem, vmem),
        scratch_shapes=scratch,
        compiler_params=pltpu.CompilerParams(
            collective_id=0, has_side_effects=True, vmem_limit_bytes=62 * 1024 * 1024
        ),
        name="learner_step",
    )(observations.reshape(TR, FB), next_observations, trunk_weights, head_weights, acting, actions, rewards, finished)


def solution(mesh):
    split = Mesh(mesh.devices.reshape(SIZES), AXES)
    return jax.shard_map(
        per_device,
        mesh=split,
        in_specs=(
            P(DP, None, GROUP),
            P(DP, GROUP),
            P(None, DP, GROUP),
            P(GROUP, None),
            P(DP, None, None),
            P(DP, None),
            P(DP, None),
            P(DP, None),
        ),
        out_specs=(P(None, DP, GROUP), P(GROUP + DP, None), P(DP, None)),
        check_vma=False,
    )
```

time: 365 us -> 165 us (0.45)
  Pallas kernels: 0 us -> 155 us
  blocking collectives: 148 us -> 0 us
  waiting for transfers between devices: 111 us -> 0 us
  matrix products: 29.5 us -> 0 us
  starting transfers between devices: 24.5 us -> 0 us
  other arithmetic: 18.2 us -> 0 us
  between operations: 14 us -> 0.65 us
  local copies, waits for them, and re-layouts: 18 us -> 7.6 us
    pallas_call x0 -> x1, Pallas kernels: none -> 155 us  [per_device(): pl.pallas_call(kernel, out_shape=(jax.ShapeDtypeStruct((2, WB, FB), F32),...]
    all_to_all x6 -> x0, blocking collectives: 148 us -> none  [the longest x4 128 us: from_everyone(): lax.all_to_all(jnp.broadcast_to(array[None], (size, *array.shape)), axis,...]
    all_to_all x4 -> x0, waiting for transfers between devices: 54.7 us -> none  [the longest x2 45.6 us: sum_in_two_steps(): lax.all_to_all(nearer.astype(jnp.bfloat16), far, split_axis=0, concat_axi...]
    all_gather x2 -> x0, waiting for transfers between devices: 29.5 us -> none  [per_device(): forward_whole = lax.all_gather(current, 'group', axis=1, tiled=True)]
    dot_general x8 -> x0, matrix products: 29.5 us -> none  [the longest x2 14.3 us: per_device(): jnp.dot(forward_whole, gathered_weights[forward_layer_index], preferred_e...]
    reduce_scatter x1 -> x0, waiting for transfers between devices: 26.5 us -> none  [per_device(): lax.psum_scatter(full_grad.astype(jnp.bfloat16), 'group', scatter_dimensi...]
    all_to_all x4 -> x0, starting transfers between devices: 24.4 us -> none  [the longest x2 11.3 us: sum_in_two_steps(): lax.all_to_all(nearer.astype(jnp.bfloat16), far, split_axis=0, concat_axi...]
    reduce_sum x9 -> x0, other arithmetic: 12.9 us -> none  [the longest x2 9.95 us: sent_and_summed(): return arrived.astype(jnp.float32).sum(axis=0)]
  transfers between devices with their start and end apart: 7 -> 0, of which waited for: 6 -> 0; matrix products, arithmetic and copies ran while one was open for 9% -> 0% of each run, Pallas kernels for 0% -> 0%
where the time goes in v1:
time: 165 us; the launch traced here: 163 us
  Pallas kernels  155 us (94%)
  local copies, waits for them, and re-layouts  7.6 us (5%)
    pallas_call x1, Pallas kernels, per_device(): pl.pallas_call(kernel, out_shape=(jax.ShapeDtypeStruct((2, WB, FB), F32),...  155 us
    unnamed x5, local copies, waits for them, and re-layouts  4.68 us

profile of v1, /device:TPU:0, one launch (start us, length us, event | category | flops | bytes accessed | tf_op | source)
XLA Modules:
  0.0 163.1 jit_solution(5960133418656101751)
XLA Ops:
  0.6 0.0 copy-start
  0.6 1.5 copy.11.head
  2.2 0.0 copy-done
  2.2 0.9 copy.12.acting
  3.1 154.8 %learner_step.1 = (f32[2,256,512]{2,1,0:T(8,128)}, f32[32,19]{1,0:T(8,128)}, f32[128,18]{1,0:T(8,128)}) custom-call(bf16[512,512]{1,0:T(8,128)(2,1)} %bitcast.1, bf16[128,512]{1,0:T(8,128)(2,1)} %nxt.1, bf16[2,256,512]{2,1,0:T(8,128)(2,1)} %wts.1, bf16[512,19]{1,0:T(8,128)(2,1)} %copy.11.head, f32[8,63,18]{2,1,0:T(8,128)} %copy.12.acting, s32[8,63]{1,0:T(8,128)} %actions.1, ...), custom_call_target="tpu_custom_call" | custom-call | tf_op jit(solution)/shard_map/learner_step/pallas_call | solution.py:614
  157.9 1.4 copy.13
  159.3 1.5 copy.14
  160.8 2.3 %copy.16 = f32[2,256,512]{2,1,0:T(8,128)} copy(f32[2,256,512]{2,1,0:T(8,128)} %get-tuple-element.9) | data formatting | bytes 2097152
Async XLA Ops:
  0.6 1.6 copy-start

commit v2 on v1

--- a/solution.py
+++ b/solution.py
@@ -306,25 +306,22 @@
     loads[2].wait()
     loads[3].wait()
 
-    tmp[...] = jnp.zeros_like(tmp)
-    tmp[:, 0 : ACT + 1] = head[...].astype(F32)
-    headt[...] = tmp[...].T.astype(BF16)
-    tmp[0:128, :] = jnp.zeros((128, 128), F32)
-    tmp[0 : STEPS - 1, 0:ACT] = acting[g]
+    headt[...] = jnp.zeros_like(headt)
+    headt[0 : ACT + 1, :] = head[...]
     misc[...] = jnp.zeros_like(misc)
-    misc[0:24, :] = tmp[0:128, :].T[0:24, :]
+    misc[0:ACT, 0 : STEPS - 1] = acting[:, pl.ds(g, 1), :].reshape(ACT, STEPS - 1)
     misc[24:25, 0 : STEPS - 1] = actions[pl.ds(g, 1), :].astype(F32)
     misc[25:26, 0 : STEPS - 1] = rewards[pl.ds(g, 1), :]
     misc[26:27, 0 : STEPS - 1] = finished[pl.ds(g, 1), :].astype(F32)
     hs[...] = jnp.zeros_like(hs)
-    tmp[0:128, :] = jnp.zeros((128, 128), F32)
+    tmp[...] = jnp.zeros_like(tmp)
 
     w_fwd1(w0)
     x_fwd1(t0)
     x_fwd2(t0)
     w_fwd2(w0)
+    x_fwd3(t0)
     w_fwd3(w0)
-    x_fwd3(t0)
     w_finish(w0)
     w1 = w_start(1)
     x_near(t0)
@@ -371,7 +368,7 @@
         total = total + hr[(g + 8 - k) % 8]
     grad = vtrace(total, misc[0:24, :], misc[24:25, :], misc[25:26, :], misc[26:27, :])
     tmp[0:24, :] = grad
-    og_s[...] = tmp[0:128, :].T[0:STEPS, :].astype(BF16)
+    og_s[...] = tmp[...].T[0:STEPS, :].astype(BF16)
     og_r[g] = og_s[...]
     outs = []
     for k in range(1, 8):
@@ -423,7 +420,7 @@
     def dw_block(i):
         return ((xh + 1 - i % 2) % 2) * 4 + (z + 2 + i // 2) % 4
 
-    def dw_open(layer, pg, dws, dwr, extra):
+    def dw_parts(layer, pg, dws, dwr, q, extra):
         base = count[0]
         count[0] += 8
         other = pl.multiple_of((1 - c) * WB, WB)
@@ -434,20 +431,15 @@
                 device_id=sibling, device_id_type=MESH,
             )
 
-        def body(i, carry):
+        def give(i, carry):
             block = dw_block(i)
-            term = tn(xf[layer][block, 0:TR, pl.ds(other, WB)], pg[...])
-            dws[i, 0:WB, :] = term.astype(BF16)
+            dws[i, 0:WB, :] = tn(xf[layer][block, 0:TR, pl.ds(other, WB)], pg[...]).astype(BF16)
             if extra:
                 head_rows(dws, i, block, 1 - c)
             copy_of(i).start()
             return carry
 
-        lax.fori_loop(0, 8, body, 0)
-        return copy_of
-
-    def dw_close(layer, pg, copy_of, dwr, q, extra):
-        def body(i, carry):
+        def keep(i, carry):
             block = dw_block(i)
             term = tn(xf[layer][block, 0:TR, pl.ds(cb, WB)], pg[...])
             copy_of(i).wait_recv()
@@ -457,7 +449,19 @@
                 q[i, WB:ER, :] = (q[i, WB:ER, :].astype(F32) + dwr[i, WB:ER, :].astype(F32)).astype(BF16)
             return carry
 
-        lax.fori_loop(0, 8, body, 0)
+        return give, keep, copy_of
+
+    def dw_run(layer, pg, dws, dwr, q, rz1, rz2, extra, size):
+        give, keep, copy_of = dw_parts(layer, pg, dws, dwr, q, extra)
+        lax.fori_loop(0, 4, give, 0)
+        lax.fori_loop(0, 2, keep, 0)
+        st = z_first(q, rz1, size)
+        lax.fori_loop(4, 8, give, 0)
+        lax.fori_loop(2, 4, keep, 0)
+        lax.fori_loop(6, 8, keep, 0)
+        z_plain(st, q, rz2, size)
+        lax.fori_loop(4, 6, keep, 0)
+        return st, copy_of
 
     def z_first(q, rz1, size):
         low, high = pl.ds(0, 128), pl.ds(128, size - 128)
@@ -491,12 +495,9 @@
         return q[4 + xr].astype(F32) + rz2[xr, 0].astype(F32) + rz2[xr, 1].astype(F32)
 
     hgp[...] = tn(x2[0:TR, :], og_r[...].reshape(TR, 128))
-    copy1 = dw_open(1, pg1, dws1, dwr1, True)
     make(5)
     make(6)
-    dw_close(1, pg1, copy1, dwr1, q1, True)
-    st1 = z_first(q1, rz1a, ER)
-    z_plain(st1, q1, rz2a, ER)
+    st1, copy1 = dw_run(1, pg1, dws1, dwr1, q1, rz1a, rz2a, True, ER)
     for rows in (lo, hi):
         own[rows, :] = piece(g, rows)
 
@@ -544,10 +545,7 @@
     a1 = x_start(1, TR, AR)
     x_own(a1, "lo")
     x_own(a1, "hi")
-    copy0 = dw_open(0, pg0, dws0, dwr0, False)
-    dw_close(0, pg0, copy0, dwr0, q0, False)
-    st0 = z_first(q0, rz1b, WB)
-    z_plain(st0, q0, rz2b, WB)
+    st0, copy0 = dw_run(0, pg0, dws0, dwr0, q0, rz1b, rz2b, False, WB)
 
     x_fwd1(a1)
     x_fwd2(a1)
@@ -555,8 +553,9 @@
     h1.wait_recv()
     value = value + rx1[...].astype(F32)
     dw_out[1] = value[0:WB, :]
-    hg_out[0:16, :] = value[WB:ER, 0 : ACT + 1]
-    hg_out[16:32, :] = value[WB:ER, 128 : 128 + ACT + 1]
+    tmp[0:16, :] = value[WB:ER, 0:128]
+    tmp[16:32, :] = value[WB:ER, 128:256]
+    hg_out[...] = tmp[...].T[0 : ACT + 1, 0:32]
     z_added(st0, q0, rz1b, rz2b, WB)
     x_fwd3(a1)
     x_near(a1)
@@ -576,8 +575,7 @@
     total = ha_s[...]
     for k in range(1, 8):
         total = total + ha_r[(g + 8 - k) % 8]
-    tmp[0:24, :] = total
-    al_out[...] = tmp[0:128, :].T[:, 0:ACT]
+    al_out[...] = total[0:ACT, :]
     value = z_sum(st0, 1, q0, rz2b)
     h0.wait_recv()
     dw_out[0] = value + rx0[...].astype(F32)
@@ -602,7 +600,7 @@
     scratch = [
         v((8, TR + AR, FB), BF16), v((8, TR + AR, FB), BF16), v((8, FB, FB), BF16), v((8, FB, FB), BF16),
         v((TR + AR, FB), F32), v((TR, FB), F32), v((TR, FB), F32), v((TR + AR, FB), BF16),
-        v((128, FB), BF16), v((FB, 128), F32), v((32, 128), F32),
+        v((128, FB), BF16), v((128, 128), F32), v((32, 128), F32),
         v((8, 24, 128), F32), v((8, 24, 128), F32), v((24, 128), F32), v((8, 24, 128), F32),
         v((STEPS, 128), BF16), v((8, STEPS, 128), BF16), v((TR, FB), BF16), v((TR, FB), BF16), v((FB, 128), F32),
         v((7, TR, FB), BF16), v((7, TR, FB), BF16), v((TR, FB), F32),
@@ -611,12 +609,12 @@
     ]
     hbm = pl.BlockSpec(memory_space=pltpu.HBM)
     vmem = pl.BlockSpec(memory_space=pltpu.VMEM)
-    return pl.pallas_call(
+    trunk_grads, head_grads, actor_logits = pl.pallas_call(
         kernel,
         out_shape=(
             jax.ShapeDtypeStruct((2, WB, FB), F32),
-            jax.ShapeDtypeStruct((32, ACT + 1), F32),
-            jax.ShapeDtypeStruct((AR, ACT), F32),
+            jax.ShapeDtypeStruct((ACT + 1, 32), F32),
+            jax.ShapeDtypeStruct((ACT, AR), F32),
         ),
         in_specs=[hbm, hbm, hbm, vmem, vmem, vmem, vmem, vmem],
         out_specs=(vmem, vmem, vmem),
@@ -625,7 +623,11 @@
             collective_id=0, has_side_effects=True, vmem_limit_bytes=62 * 1024 * 1024
         ),
         name="learner_step",
-    )(observations.reshape(TR, FB), next_observations, trunk_weights, head_weights, acting, actions, rewards, finished)
+    )(
+        observations.reshape(TR, FB), next_observations, trunk_weights, head_weights.T, acting.transpose(2, 0, 1),
+        actions, rewards, finished,
+    )
+    return trunk_grads, head_grads.T, actor_logits.T
 
 
 def solution(mesh):

time: 165 us -> 156 us (0.945)
  local copies, waits for them, and re-layouts: 7.6 us -> 3.58 us
  Pallas kernels: 155 us -> 151 us
    pallas_call x1, Pallas kernels: 155 us -> 151 us  [per_device(): pl.pallas_call(kernel, out_shape=(jax.ShapeDtypeStruct((2, WB, FB), F32),...]
    pallas_call x2 -> x0, local copies, waits for them, and re-layouts: 2.91 us -> none  [per_device(): pl.pallas_call(kernel, out_shape=(jax.ShapeDtypeStruct((2, WB, FB), F32),...]
    unnamed x5 -> x7, local copies, waits for them, and re-layouts: 4.68 us -> 3.58 us
where the time goes in v2:
time: 156 us
  Pallas kernels  151 us (97%)
  local copies, waits for them, and re-layouts  3.58 us (2%)
    pallas_call x1, Pallas kernels, per_device(): pl.pallas_call(kernel, out_shape=(jax.ShapeDtypeStruct((2, WB, FB), F32),...  151 us
    unnamed x7, local copies, waits for them, and re-layouts  3.58 us

profile of v2, /device:TPU:0, one launch (start us, length us, event | category | flops | bytes accessed | tf_op | source)
XLA Modules:
  0.0 155.7 jit_solution(896438562474937392)
XLA Ops:
  0.6 151.4 %learner_step.1 = (f32[2,256,512]{2,1,0:T(8,128)}, f32[19,32]{1,0:T(8,128)}, f32[18,128]{1,0:T(8,128)}) custom-call(bf16[512,512]{1,0:T(8,128)(2,1)} %bitcast.5, bf16[128,512]{1,0:T(8,128)(2,1)} %nxt.1, bf16[2,256,512]{2,1,0:T(8,128)(2,1)} %wts.1, bf16[19,512]{1,0:T(8,128)(2,1)} %bitcast.7, f32[18,8,63]{2,1,0:T(8,128)} %bitcast.6, s32[8,63]{1,0:T(8,128)} %actions.1, ...), custom_call_target="tpu_custom_call" | custom-call | tf_op jit(solution)/shard_map/learner_step/pallas_call | solution.py:612
  152.1 0.0 copy-start.1
  152.1 2.3 %copy.14 = f32[2,256,512]{2,1,0:T(8,128)} copy(f32[2,256,512]{2,1,0:T(8,128)} %get-tuple-element.12) | data formatting | bytes 2097152
  154.3 0.0 copy-done.1
  154.4 0.0 copy-start
  154.4 0.6 copy.15
  155.0 0.1 copy-done
  155.1 0.6 copy.16
Async XLA Ops:
  152.1 2.3 %copy-start.1 = (f32[19,32]{1,0:T(8,128)S(1)}, f32[19,32]{1,0:T(8,128)}, u32[]{:S(2)}) copy-start(f32[19,32]{1,0:T(8,128)} %get-tuple-element.7) | copy-start | bytes 7300
  154.4 0.7 copy-start

commit v3 on v2

v3 whole, which is shorter than its diff:
```python
import functools

import jax
import jax.numpy as jnp
from jax import lax
from jax.experimental import pallas as pl
from jax.experimental.pallas import tpu as pltpu
from jax.sharding import Mesh
from jax.sharding import PartitionSpec as P

AXES = ("xl", "y", "xh", "z", "c")
SIZES = (2, 4, 2, 4, 2)
DP = ("xh", "z", "c")
GROUP = ("xl", "y")
MESH = pl.DeviceIdType.MESH
F32 = jnp.float32
BF16 = jnp.bfloat16

discount_rate = 0.99
value_weight = 0.5
entropy_weight = 0.1
loss_divisor = 16.0

TR = 512
AR = 128
FB = 512
WB = 256
STEPS = 64
ACT = 18
ER = 544
N_RECV, N_SEND = 148, 21
CH = 256


def nn(a, b):
    return jnp.dot(a, b, preferred_element_type=F32)


def nt(a, b):
    return lax.dot_general(a, b, (((1,), (1,)), ((), ())), preferred_element_type=F32)


def tn(a, b):
    return lax.dot_general(a, b, (((0,), (0,)), ((), ())), preferred_element_type=F32)


def vtrace(logits, behave, action, reward, finished):
    row = lax.broadcasted_iota(jnp.int32, logits.shape, 0)
    step = lax.broadcasted_iota(jnp.int32, reward.shape, 1)
    live = step % STEPS < STEPS - 1
    lanes = reward.shape[1]
    is_act = row < ACT

    def log_softmax(values):
        top = jnp.max(jnp.where(is_act, values, -3.0e38), axis=0, keepdims=True)
        shifted = jnp.where(is_act, values - top, 0.0)
        total = jnp.sum(jnp.where(is_act, jnp.exp(shifted), 0.0), axis=0, keepdims=True)
        return jnp.where(is_act, shifted - jnp.log(total), 0.0)

    log_policy = log_softmax(logits)
    log_behave = log_softmax(behave)
    chosen = jnp.where(row.astype(F32) == action, 1.0, 0.0)
    ratio = jnp.exp(jnp.sum((log_policy - log_behave) * chosen, axis=0, keepdims=True))
    clipped = jnp.minimum(ratio, 1.0)
    discount = discount_rate * (1.0 - finished)
    current = logits[ACT : ACT + 1, :]
    following = pltpu.roll(current, lanes - 1, 1)
    delta = jnp.where(live, clipped * (reward + discount * following - current), 0.0)
    factor = jnp.where(live, discount * clipped, 0.0)
    for shift in (1, 2, 4, 8, 16, 32):
        delta = delta + factor * pltpu.roll(delta, lanes - shift, 1)
        factor = factor * pltpu.roll(factor, lanes - shift, 1)
    targets = current + delta
    next_targets = pltpu.roll(targets, lanes - 1, 1)
    advantage = clipped * (reward + discount * next_targets - current)
    probability = jnp.where(is_act, jnp.exp(log_policy), 0.0)
    entropy = -jnp.sum(probability * log_policy, axis=0, keepdims=True)
    logit_grad = (
        -advantage * (chosen - probability)
        + entropy_weight * probability * (log_policy + entropy)
    ) / loss_divisor
    value_grad = -value_weight * (targets - current) / loss_divisor
    grad = jnp.where(is_act, logit_grad, jnp.where(row == ACT, value_grad, 0.0))
    return jnp.where(live, grad, 0.0)


def kernel(
    obs, nxt, wts, head, acting, actions, rewards, finished,
    dw_out, hg_out, al_out,
    xf0, xf1, wf0, wf1, acc, slope0, slope1, x2, headt, tmp, misc,
    hs, hr, ha_s, ha_r, og_r, pg1, pg1t, pg0t, hgp,
    sb, rb, own,
    dws1, dwr1, q1, rz1a, rz2a, xs1, rx1,
    dws0, dwr0, q0, rz1b, rz2b, xs0, rx0, rxx,
    ssem, rsem, lsem,
):
    xl, y, xh, z, c = (lax.axis_index(a) for a in AXES)
    g = xl * 4 + y
    xf, wf = (xf0, xf1), (wf0, wf1)

    def rel_g(dx, dy):
        return ((xl + dx) % 2) * 4 + (y + dy) % 4

    def rel_w(dx, dz):
        return ((xh + dx) % 2) * 4 + (z + dz) % 4

    x_peer = {"xl": 1 - xl}
    y_up, y_down = {"y": (y + 1) % 4}, {"y": (y + 3) % 4}
    h_peer = {"xh": 1 - xh}
    z_up, z_down = {"z": (z + 1) % 4}, {"z": (z + 3) % 4}
    sibling = {"c": 1 - c}

    count = [0, 0]
    sends = []

    def new_recv():
        count[0] += 1
        return rsem.at[count[0] - 1]

    def new_send(view):
        count[1] += 1
        sem = ssem.at[count[1] - 1]
        sends.append((view, sem))
        return sem

    class Recv:
        def __init__(self, sem, view):
            self.sem, self.view = sem, view

        def wait_recv(self):
            pltpu.make_async_remote_copy(
                src_ref=self.view, dst_ref=self.view, send_sem=ssem.at[0], recv_sem=self.sem,
                device_id=x_peer, device_id_type=MESH,
            ).wait_recv()

    def send(src, dst, device, send_sem, recv_sem=None):
        copy = pltpu.make_async_remote_copy(
            src_ref=src, dst_ref=dst, send_sem=send_sem, recv_sem=new_recv() if recv_sem is None else recv_sem,
            device_id=device, device_id_type=MESH,
        )
        copy.start()
        return copy

    cb = pl.multiple_of(c * WB, WB)
    wg = xh * 4 + z
    loads = [
        pltpu.make_async_copy(obs, xf0.at[g, pl.ds(0, TR), :], lsem.at[0]),
        pltpu.make_async_copy(wts.at[0], wf0.at[wg, pl.ds(cb, WB), :], lsem.at[1]),
        pltpu.make_async_copy(wts.at[1], wf1.at[wg, pl.ds(cb, WB), :], lsem.at[2]),
        pltpu.make_async_copy(nxt, xf0.at[g, pl.ds(TR, AR), :], lsem.at[3]),
    ]
    for load in loads:
        load.start()

    barrier = pltpu.get_barrier_semaphore()
    friends = [h_peer, z_up, z_down, sibling]
    for k in range(1, 8):
        gt = (g + k) % 8
        friends.append({"xl": gt // 4, "y": gt % 4})
    for friend in friends:
        pl.semaphore_signal(barrier, inc=1, device_id=friend, device_id_type=MESH)
    pl.semaphore_wait(barrier, len(friends))

    def x_start(layer, first, amount):
        buf, half = xf[layer], amount // 2
        lo, hi = pl.ds(first, half), pl.ds(first + half, half)

        out = new_send(buf.at[pl.ds(0, 7), pl.ds(0, amount), :])

        def go(block, rows, device, recv_sem=None):
            return send(buf.at[block, rows, :], buf.at[block, rows, :], device, out, recv_sem)

        near = Recv(new_recv(), buf.at[0, pl.ds(0, amount), :])
        far = Recv(new_recv(), buf.at[pl.ds(0, 3), pl.ds(0, amount), :])
        return {"go": go, "lo": lo, "hi": hi, "near": near, "far": far}

    def x_own(st, rows):
        go, lo = st["go"], st["lo"]
        if rows == "lo":
            st["up_lo"] = go(g, lo, y_up)
            st["x_lo"] = go(g, lo, x_peer)
        else:
            st["dn_hi"] = go(g, st["hi"], y_down)
            st["x_hi"] = go(g, st["hi"], x_peer)
            go(g, st["hi"], y_up, st["near"].sem)
            go(g, lo, y_down, st["near"].sem)

    def x_fwd1(st):
        go = st["go"]
        st["up_lo"].wait_recv()
        st["f_lo"] = go(rel_g(0, 3), st["lo"], y_up)
        st["dn_hi"].wait_recv()
        st["f_hi"] = go(rel_g(0, 1), st["hi"], y_down)

    def x_fwd2(st):
        go, block, far = st["go"], rel_g(1, 0), st["far"].sem
        st["x_lo"].wait_recv()
        go(block, st["lo"], y_up, far)
        go(block, st["lo"], y_down, far)
        st["x_hi"].wait_recv()
        go(block, st["hi"], y_up, far)
        go(block, st["hi"], y_down, far)

    def x_fwd3(st):
        go, block, far = st["go"], rel_g(0, 2), st["far"].sem
        st["f_lo"].wait_recv()
        go(block, st["lo"], x_peer, far)
        st["f_hi"].wait_recv()
        go(block, st["hi"], x_peer, far)

    def x_near(st):
        st["near"].wait_recv()

    def x_far(st):
        st["far"].wait_recv()

    half_w = WB // 2

    def w_piece(block, part):
        if part == "all":
            return (block, pl.ds(cb, WB), slice(None))
        start = cb if part == "lo" else cb + half_w
        return (block, pl.ds(pl.multiple_of(start, half_w), half_w), slice(None))

    def w_start(layer):
        buf = wf[layer]

        out = new_send(xf[layer].at[pl.ds(0, 6), :, :])

        def go(block, part, device, recv_sem=None):
            where = w_piece(block, part)
            return send(buf.at[where], buf.at[where], device, out, recv_sem)

        st = {"go": go}
        st["f"] = Recv(new_recv(), buf.at[0, pl.ds(0, WB), :])
        st["g"] = Recv(new_recv(), buf.at[0, pl.ds(0, WB), :])
        st["sib"] = Recv(new_recv(), buf.at[pl.ds(0, 4), :, :])
        st["up_lo"] = go(wg, "lo", z_up)
        st["dn_hi"] = go(wg, "hi", z_down)
        st["h"] = go(wg, "all", h_peer)
        st["up_hi"] = go(wg, "hi", z_up)
        st["dn_lo"] = go(wg, "lo", z_down)
        w_share(st, wg)
        return st

    def w_share(st, block):
        st["go"](block, "all", sibling, st["sib"].sem)

    def w_fwd1(st):
        go = st["go"]
        st["up_lo"].wait_recv()
        go(rel_w(0, 3), "lo", z_up, st["f"].sem)
        st["dn_hi"].wait_recv()
        go(rel_w(0, 1), "hi", z_down, st["f"].sem)

    def w_fwd2(st):
        go, far = st["go"], rel_w(1, 0)
        st["h"].wait_recv()
        st["h_up_lo"] = go(far, "lo", z_up)
        st["h_dn_hi"] = go(far, "hi", z_down)
        st["h_up_hi"] = go(far, "hi", z_up)
        st["h_dn_lo"] = go(far, "lo", z_down)
        w_share(st, far)
        st["up_hi"].wait_recv()
        w_share(st, rel_w(0, 3))
        st["dn_lo"].wait_recv()
        w_share(st, rel_w(0, 1))

    def w_fwd3(st):
        go = st["go"]
        st["h_up_lo"].wait_recv()
        go(rel_w(1, 3), "lo", z_up, st["g"].sem)
        st["h_dn_hi"].wait_recv()
        go(rel_w(1, 1), "hi", z_down, st["g"].sem)
        st["f"].wait_recv()
        w_share(st, rel_w(0, 2))

    def w_finish(st):
        st["h_up_hi"].wait_recv()
        w_share(st, rel_w(1, 3))
        st["h_dn_lo"].wait_recv()
        w_share(st, rel_w(1, 1))
        st["g"].wait_recv()
        w_share(st, rel_w(1, 2))
        st["sib"].wait_recv()

    def blocks(layer, first, amount, j0, j1, fresh):
        buf, weights = xf[layer], wf[layer]
        rows = slice(first, first + amount)
        if fresh:
            acc[rows, :] = nn(buf[g, rows, :], weights[g])

        def body(j, carry):
            block = ((xl + j // 4) % 2) * 4 + (y + j % 4) % 4
            acc[rows, :] += nn(buf[block, rows, :], weights[block])
            return carry

        lax.fori_loop(j0, j1, body, 0)

    def activate(first, amount, out, slope, tile=64):
        def body(i, carry):
            rows = pl.ds(pl.multiple_of(first + i * tile, tile), tile)
            value = acc[rows, :]
            sigma = jax.nn.sigmoid(value)
            out(rows, (value * sigma).astype(BF16))
            if slope is not None:
                slope[rows, :] = sigma * (1.0 + value * (1.0 - sigma))
            return carry

        lax.fori_loop(0, amount // tile, body, 0)

    def into_x1(rows, value):
        xf1[g, rows, :] = value

    def into_x2(rows, value):
        x2[rows, :] = value

    def next_layer(first, slope):
        st = x_start(1, first, CH)
        activate(first, CH // 2, into_x1, slope)
        x_own(st, "lo")
        activate(first + CH // 2, CH // 2, into_x1, slope)
        x_own(st, "hi")
        return st

    def to_group(src, dst, landed):
        out, got = new_send(landed), new_recv()
        for k in range(1, 8):
            gt = (g + k) % 8
            send(src, dst.at[g], {"xl": gt // 4, "y": gt % 4}, out, got)
        return Recv(got, landed)

    def from_group(own_part, dst):
        total = own_part[...]
        for k in range(1, 8):
            total = total + dst[(g + 8 - k) % 8]
        return total

    def head_send(ch):
        hs[ch] = nt(headt[0:32, :], x2[CH * ch : CH * (ch + 1), :])[0:24, :]
        return to_group(hs.at[ch], hr.at[ch], hr.at[ch, pl.ds(0, 7), :, :])

    def head_loss(ch, got):
        got.wait_recv()
        total = from_group(hs.at[ch], hr.at[ch])
        grad = vtrace(total, misc[ch, 0:24, :], misc[ch, 24:25, :], misc[ch, 25:26, :], misc[ch, 26:27, :])
        tmp[0:24, :] = grad
        rows = slice(CH * ch, CH * (ch + 1))
        og_r[rows, :] = tmp[...].T.astype(BF16)
        pg1[rows, :] = (nn(og_r[rows, :], headt[...]) * slope1[rows, :]).astype(BF16)
        pg1t[:, rows] = pg1[rows, :].T

    where_g = (rel_g(1, 2), rel_g(1, 1), rel_g(1, 3), rel_g(0, 1), rel_g(0, 3), rel_g(0, 2), rel_g(1, 0))

    class Scatter:
        def __init__(self, first, amount, col, cols):
            half = amount // 2
            self.rows = slice(first, first + amount)
            self.lo, self.hi = slice(first, first + half), slice(first + half, first + amount)
            self.cs = slice(col, col + cols)
            self.out = new_send(sb.at[:, self.ds(self.rows), self.ds(self.cs)])
            self.s2 = [Recv(new_recv(), rb.at[pl.ds(0, 2), self.ds(rows), self.ds(self.cs)]) for rows in (self.lo, self.hi)]
            self.last = Recv(new_recv(), rb.at[pl.ds(0, 3), self.ds(self.rows), self.ds(self.cs)])

        def ds(self, rows):
            return pl.ds(rows.start, rows.stop - rows.start)

        def piece(self, block):
            return nt(pg1[self.rows, :], wf1[block, self.cs, :])

        def make(self, k):
            sb[k, self.rows, self.cs] = self.piece(where_g[k]).astype(BF16)

        def push(self, k, rows, device, recv_sem=None):
            where = (k, self.ds(rows), self.ds(self.cs))
            return send(sb.at[where], rb.at[where], device, self.out, recv_sem)

        def add_in(self, k, rows, *terms):
            value = sb[k, rows, self.cs].astype(F32)
            for term in terms:
                value = value + rb[term, rows, self.cs].astype(F32)
            sb[k, rows, self.cs] = value.astype(BF16)

        def make_all(self):
            self.make(0)
            self.s1 = [self.push(0, self.lo, x_peer), self.push(0, self.hi, x_peer)]
            for k in range(1, 7):
                self.make(k)
            own[self.rows, self.cs] = self.piece(g)

        def push_y(self):
            for i, rows in enumerate((self.lo, self.hi)):
                self.push(1, rows, y_up, self.s2[i].sem)
                self.push(2, rows, y_down, self.s2[i].sem)
            self.push(3, self.hi, y_up, self.last.sem)
            self.push(4, self.lo, y_down, self.last.sem)

        def mid1(self):
            self.s1[0].wait_recv()
            self.add_in(5, self.lo, 0)
            self.s4u = self.push(5, self.lo, y_up)
            self.s1[1].wait_recv()
            self.add_in(5, self.hi, 0)
            self.s4d = self.push(5, self.hi, y_down)

        def mid2(self):
            for i, rows in enumerate((self.lo, self.hi)):
                self.s2[i].wait_recv()
                self.add_in(6, rows, 1, 2)
                self.push(6, rows, x_peer, self.last.sem)

        def mid3(self):
            self.s4u.wait_recv()
            self.add_in(3, self.lo, 5)
            self.push(3, self.lo, y_up, self.last.sem)
            self.s4d.wait_recv()
            self.add_in(4, self.hi, 5)
            self.push(4, self.hi, y_down, self.last.sem)

        def close(self):
            self.last.wait_recv()
            cs = self.cs
            for r in range(self.rows.start, self.rows.stop, 128):
                rows = slice(r, r + 128)
                value = own[rows, cs] + rb[3, rows, cs].astype(F32) + rb[4, rows, cs].astype(F32) + rb[6, rows, cs].astype(F32)
                pg0t[cs, rows] = (value * slope0[rows, cs]).astype(BF16).T

    class Weights:
        def __init__(self, layer, pgt, bufs, col, cols, extra, halves=(0, 1)):
            self.halves = halves
            self.layer, self.pgt, self.extra = layer, pgt, extra
            self.dws, self.dwr, self.q, self.rz1, self.rz2, self.xs, self.rx = bufs
            self.cols, self.size = cols, cols + extra
            self.cs, self.top = slice(col, col + cols), slice(col + cols, col + cols + extra)
            self.all, half = slice(col, col + self.size), col + cols // 2
            self.low, self.high = slice(col, half), slice(half, col + self.size)
            self.base = count[0]
            count[0] += 8
            every = self.ds(self.all)
            self.out = new_send(self.q.at[pl.ds(0, 7), every, :])
            self.give_sem = new_send(self.dws.at[:, every, :])
            self.sums = {xr: Recv(new_recv(), self.rz2.at[xr, :, every, :]) for xr in halves}
            self.st = {}

        def ds(self, rows):
            return pl.ds(rows.start, rows.stop - rows.start)

        def block(self, i):
            return ((xh + 1 - i % 2) % 2) * 4 + (z + 2 + i // 2) % 4

        def copy_of(self, i):
            every = self.ds(self.all)
            return pltpu.make_async_remote_copy(
                src_ref=self.dws.at[i, every, :], dst_ref=self.dwr.at[i, every, :],
                send_sem=self.give_sem, recv_sem=rsem.at[self.base + i],
                device_id=sibling, device_id_type=MESH,
            )

        def head_rows(self, block, core):
            return hgp[pl.ds(pl.multiple_of((2 * block + core) * 32, 32), 32), :]

        def give(self, i0, i1):
            other = pl.multiple_of((1 - c) * WB, WB)

            def body(i, carry):
                block = self.block(i)
                term = nn(self.pgt[self.cs, :], xf[self.layer][block, 0:TR, pl.ds(other, WB)])
                self.dws[i, self.cs, :] = term.astype(BF16)
                if self.extra:
                    self.dws[i, self.top, 0:128] = self.head_rows(block, 1 - c).astype(BF16)
                    self.dws[i, self.top, 128:256] = jnp.zeros((self.extra, 128), BF16)
                self.copy_of(i).start()
                return carry

            lax.fori_loop(i0, i1, body, 0)

        def keep(self, i0, i1):
            q, dwr, cs, top = self.q, self.dwr, self.cs, self.top

            def body(i, carry):
                block = self.block(i)
                term = nn(self.pgt[cs, :], xf[self.layer][block, 0:TR, pl.ds(cb, WB)])
                self.copy_of(i).wait_recv()
                q[i, cs, :] = (term + dwr[i, cs, :].astype(F32)).astype(BF16)
                if self.extra:
                    q[i, top, 0:128] = (self.head_rows(block, c) + dwr[i, top, 0:128].astype(F32)).astype(BF16)
                    q[i, top, 128:256] = jnp.zeros((self.extra, 128), BF16)
                return carry

            lax.fori_loop(i0, i1, body, 0)

        def go(self, i, rows, dst, device, recv_sem=None):
            where = self.ds(rows)
            return send(self.q.at[i, where, :], dst.at[where, :], device, self.out, recv_sem)

        def z_first(self):
            for xr in self.halves:
                self.st["a", xr] = self.go(xr, self.low, self.rz1.at[xr], z_up)
                self.st["b", xr] = self.go(xr, self.high, self.rz1.at[xr], z_down)

        def z_plain(self):
            for xr in self.halves:
                self.go(6 + xr, self.high, self.rz2.at[xr, 0], z_up, self.sums[xr].sem)
                self.go(2 + xr, self.low, self.rz2.at[xr, 1], z_down, self.sums[xr].sem)

        def early(self):
            self.give(0, 4)
            self.keep(0, 2)
            self.z_first()
            self.give(4, 8)

        def late(self):
            self.keep(2, 4)
            self.keep(6, 8)
            self.z_plain()
            self.keep(4, 6)

        def z_added(self):
            q, rz1, st = self.q, self.rz1, self.st
            for xr in self.halves:
                for name, i, rows, side, device in (("a", 6, self.low, 0, z_up), ("b", 2, self.high, 1, z_down)):
                    st[name, xr].wait_recv()
                    value = q[i + xr, rows, :].astype(F32) + rz1[xr, rows, :].astype(F32)
                    q[i + xr, rows, :] = value.astype(BF16)
                    self.go(i + xr, rows, self.rz2.at[xr, side], device, self.sums[xr].sem)

        def z_sum(self, xr):
            self.sums[xr].wait_recv()
            every = self.all
            return (
                self.q[4 + xr, every, :].astype(F32)
                + self.rz2[xr, 0, every, :].astype(F32)
                + self.rz2[xr, 1, every, :].astype(F32)
            )

        def cross(self):
            every = self.ds(self.all)
            self.xs[self.all, :] = self.z_sum(0).astype(BF16)
            self.h = send(self.xs.at[every, :], self.rx.at[every, :], h_peer, self.out)

        def x_open(self):
            self.give(0, 4)
            self.keep(0, 2)
            self.x_push(0)
            self.keep(2, 4)
            self.x_push(2)
            self.give(4, 8)
            self.keep(6, 8)
            self.x_push(6)
            self.keep(4, 6)
            self.x_push(4)

        def x_push(self, i):
            every = self.ds(self.all)
            self.st["x", i] = send(self.q.at[i, every, :], rxx.at[i // 2], h_peer, self.out)

        def x_take(self, i):
            self.st["x", i].wait_recv()
            value = self.q[i + 1, self.all, :].astype(F32) + rxx[i // 2].astype(F32)
            self.q[i + 1, self.all, :] = value.astype(BF16)

        def result(self):
            value = self.z_sum(1)
            if 0 in self.halves:
                self.h.wait_recv()
                value = value + self.rx[self.all, :].astype(F32)
            dw_out[self.layer, :, self.cs] = value[0 : self.cols, :].T
            if self.extra:
                hg_out[...] = value[self.cols :, 0:128].T[0 : ACT + 1, :]

    loads[0].wait()
    loads[1].wait()
    w0 = w_start(0)
    a0, b0 = x_start(0, 0, CH), x_start(0, CH, CH)
    x_own(a0, "lo")
    x_own(a0, "hi")
    x_own(b0, "lo")
    x_own(b0, "hi")
    loads[2].wait()
    loads[3].wait()

    headt[...] = jnp.zeros_like(headt)
    headt[0 : ACT + 1, :] = head[...]
    misc[...] = jnp.zeros_like(misc)
    for r in range(8):
        ch, lane = r // 4, STEPS * (r % 4)
        steps = slice(lane, lane + STEPS - 1)
        misc[ch, 0:ACT, steps] = acting[:, r, :]
        misc[ch, 24:25, steps] = actions[r : r + 1, :].astype(F32)
        misc[ch, 25:26, steps] = rewards[r : r + 1, :]
        misc[ch, 26:27, steps] = finished[r : r + 1, :].astype(F32)
    tmp[...] = jnp.zeros_like(tmp)

    w_fwd1(w0)
    x_fwd1(a0)
    w_fwd2(w0)
    x_fwd1(b0)
    x_fwd2(a0)
    w_fwd3(w0)
    x_fwd3(a0)
    x_fwd2(b0)
    x_fwd3(b0)
    w1 = w_start(1)
    w_finish(w0)
    x_near(a0)
    blocks(0, 0, CH, 1, 5, True)
    x_far(a0)
    blocks(0, 0, CH, 5, 8, False)
    a1 = next_layer(0, slope0)
    w_fwd1(w1)
    x_near(b0)
    blocks(0, CH, CH, 1, 5, True)
    x_far(b0)
    blocks(0, CH, CH, 5, 8, False)
    b1 = next_layer(CH, slope0)

    x_fwd1(a1)
    w_fwd2(w1)
    x_fwd1(b1)
    x_fwd2(a1)
    w_fwd3(w1)
    x_fwd3(a1)
    x_fwd3(b1)
    x_fwd2(b1)
    w_finish(w1)
    x_near(a1)
    blocks(1, 0, CH, 1, 5, True)
    x_far(a1)
    blocks(1, 0, CH, 5, 8, False)
    activate(0, CH, into_x2, slope1)
    head_a = head_send(0)
    c0 = x_start(0, TR, AR)
    x_own(c0, "lo")
    x_own(c0, "hi")
    x_near(b1)
    blocks(1, CH, CH, 1, 5, True)
    x_far(b1)
    blocks(1, CH, CH, 5, 8, False)
    activate(CH, CH, into_x2, slope1)
    head_b = head_send(1)
    x_fwd1(c0)
    x_fwd2(c0)

    da1, da2 = Scatter(0, CH, 0, CH), Scatter(0, CH, CH, CH)
    db1, db2 = Scatter(CH, CH, 0, CH), Scatter(CH, CH, CH, CH)
    g1 = Weights(1, pg1t, (dws1, dwr1, q1, rz1a, rz2a, xs1, rx1), 0, FB, ER - FB)
    bufs0 = (dws0, dwr0, q0, rz1b, rz2b, xs0, rx0)
    g0a = Weights(0, pg0t, bufs0, 0, CH, 0)
    g0b = Weights(0, pg0t, bufs0, CH, CH, 0)
    head_loss(0, head_a)
    da1.make_all()
    da1.push_y()
    da2.make_all()
    da2.push_y()
    head_loss(1, head_b)
    db1.make_all()
    db1.push_y()
    da1.mid1()
    hgp[...] = tn(x2[0:TR, :], og_r[...])
    g1.give(0, 4)
    g1.keep(0, 2)
    g1.z_first()
    da1.mid2()
    db1.mid1()
    x_fwd3(c0)
    da2.mid1()
    db2.make_all()
    db2.push_y()
    da1.mid3()
    db1.mid2()
    g1.give(4, 8)
    da2.mid2()
    g1.keep(2, 4)
    db1.mid3()
    db2.mid1()
    g1.keep(6, 8)
    g1.z_plain()
    da2.mid3()
    g1.keep(4, 6)
    db2.mid2()
    g1.z_added()
    da1.close()
    x_near(c0)
    x_far(c0)
    blocks(0, TR, AR, 1, 8, True)
    activate(TR, AR, into_x1, None)
    db1.close()
    g0a.give(0, 4)
    db2.mid3()
    c1 = x_start(1, TR, AR)
    x_own(c1, "lo")
    x_own(c1, "hi")
    g0a.keep(0, 2)
    g0a.z_first()
    g0a.give(4, 8)
    g0a.late()
    da2.close()
    x_fwd1(c1)
    x_fwd2(c1)
    db2.close()
    g0b.early()
    g0a.z_added()
    x_fwd3(c1)
    g0b.late()
    g1.cross()
    x_near(c1)
    x_far(c1)
    blocks(1, TR, AR, 1, 8, True)
    activate(TR, AR, into_x2, None)
    ha_s[...] = nt(headt[0:32, :], x2[TR : TR + AR, :])[0:24, :]
    acts = to_group(ha_s, ha_r, ha_r.at[pl.ds(0, 7), :, :])
    g0a.cross()
    g0b.z_added()
    g1.result()
    acts.wait_recv()
    al_out[...] = from_group(ha_s, ha_r)[0:ACT, :]
    g0b.cross()
    g0a.result()
    g0b.result()

    for view, sem in sends:
        pltpu.make_async_remote_copy(
            src_ref=view, dst_ref=view, send_sem=sem, recv_sem=rsem.at[0], device_id=x_peer, device_id_type=MESH,
        ).wait_send()
    assert (count[0], count[1]) == (N_RECV, N_SEND), count


def per_device(observations, next_observations, trunk_weights, head_weights, acting, actions, rewards, finished):
    v = pltpu.VMEM
    dw_bufs = lambda rows: [
        v((8, rows, WB), BF16), v((8, rows, WB), BF16), v((8, rows, WB), BF16), v((2, rows, WB), BF16),
        v((2, 2, rows, WB), BF16), v((rows, WB), BF16), v((rows, WB), BF16),
    ]
    scratch = [
        v((8, TR + AR, FB), BF16), v((8, TR + AR, FB), BF16), v((8, FB, FB), BF16), v((8, FB, FB), BF16),
        v((TR + AR, FB), F32), v((TR, FB), F32), v((TR, FB), F32), v((TR + AR, FB), BF16),
        v((128, FB), BF16), v((128, CH), F32), v((2, 32, CH), F32),
        v((2, 24, CH), F32), v((2, 8, 24, CH), F32), v((24, 128), F32), v((8, 24, 128), F32),
        v((TR, 128), BF16), v((TR, FB), BF16), v((FB, TR), BF16), v((FB, TR), BF16), v((FB, 128), F32),
        v((7, TR, FB), BF16), v((7, TR, FB), BF16), v((TR, FB), F32),
        *dw_bufs(ER), *dw_bufs(FB), v((4, CH, WB), BF16),
        pltpu.SemaphoreType.DMA((N_SEND,)), pltpu.SemaphoreType.DMA((N_RECV,)), pltpu.SemaphoreType.DMA((4,)),
    ]
    hbm = pl.BlockSpec(memory_space=pltpu.HBM)
    vmem = pl.BlockSpec(memory_space=pltpu.VMEM)
    trunk_grads, head_grads, actor_logits = pl.pallas_call(
        kernel,
        out_shape=(
            jax.ShapeDtypeStruct((2, WB, FB), F32),
            jax.ShapeDtypeStruct((ACT + 1, 32), F32),
            jax.ShapeDtypeStruct((ACT, AR), F32),
        ),
        in_specs=[hbm, hbm, hbm, vmem, vmem, vmem, vmem, vmem],
        out_specs=(vmem, vmem, vmem),
        scratch_shapes=scratch,
        compiler_params=pltpu.CompilerParams(
            collective_id=0, has_side_effects=True, vmem_limit_bytes=62 * 1024 * 1024
        ),
        name="learner_step",
    )(
        observations.reshape(TR, FB), next_observations, trunk_weights, head_weights.T, acting.transpose(2, 0, 1),
        actions, rewards, finished,
    )
    return trunk_grads, head_grads.T, actor_logits.T


def solution(mesh):
    split = Mesh(mesh.devices.reshape(SIZES), AXES)
    return jax.shard_map(
        per_device,
        mesh=split,
        in_specs=(
            P(DP, None, GROUP),
            P(DP, GROUP),
            P(None, DP, GROUP),
            P(GROUP, None),
            P(DP, None, None),
            P(DP, None),
            P(DP, None),
            P(DP, None),
        ),
        out_specs=(P(None, DP, GROUP), P(GROUP + DP, None), P(DP, None)),
        check_vma=False,
    )
```

time: 156 us -> 139 us (0.89)
  Pallas kernels: 151 us -> 134 us
    pallas_call x1, Pallas kernels: 151 us -> 134 us  [per_device(): pl.pallas_call(kernel, out_shape=(jax.ShapeDtypeStruct((2, WB, FB), F32),...]
where the time goes in v3:
time: 139 us; the launch traced here: 138 us
  Pallas kernels  134 us (96%)
  local copies, waits for them, and re-layouts  3.58 us (3%)
    pallas_call x1, Pallas kernels, per_device(): pl.pallas_call(kernel, out_shape=(jax.ShapeDtypeStruct((2, WB, FB), F32),...  134 us
    unnamed x7, local copies, waits for them, and re-layouts  3.58 us

profile of v3, /device:TPU:0, one launch (start us, length us, event | category | flops | bytes accessed | tf_op | source)
XLA Modules:
  0.0 138.4 jit_solution(15468874270588886158)
XLA Ops:
  0.6 134.2 %learner_step.1 = (f32[2,256,512]{2,1,0:T(8,128)}, f32[19,32]{1,0:T(8,128)}, f32[18,128]{1,0:T(8,128)}) custom-call(bf16[512,512]{1,0:T(8,128)(2,1)} %bitcast.5, bf16[128,512]{1,0:T(8,128)(2,1)} %nxt.1, bf16[2,256,512]{2,1,0:T(8,128)(2,1)} %wts.1, bf16[19,512]{1,0:T(8,128)(2,1)} %bitcast.7, f32[18,8,63]{2,1,0:T(8,128)} %bitcast.6, s32[8,63]{1,0:T(8,128)} %actions.1, ...), custom_call_target="tpu_custom_call" | custom-call | tf_op jit(solution)/shard_map/learner_step/pallas_call | solution.py:746
  134.8 0.0 copy-start.1
  134.8 2.3 %copy.14 = f32[2,256,512]{2,1,0:T(8,128)} copy(f32[2,256,512]{2,1,0:T(8,128)} %get-tuple-element.12) | data formatting | bytes 2097152
  137.1 0.0 copy-done.1
  137.1 0.0 copy-start
  137.1 0.6 copy.15
  137.7 0.1 copy-done
  137.8 0.6 copy.16
Async XLA Ops:
  134.8 2.3 %copy-start.1 = (f32[19,32]{1,0:T(8,128)S(1)}, f32[19,32]{1,0:T(8,128)}, u32[]{:S(2)}) copy-start(f32[19,32]{1,0:T(8,128)} %get-tuple-element.7) | copy-start | bytes 7300
  137.1 0.7 copy-start

commit v4 on v3

--- a/solution.py
+++ b/solution.py
@@ -91,7 +91,7 @@
     hs, hr, ha_s, ha_r, og_r, pg1, pg1t, pg0t, hgp,
     sb, rb, own,
     dws1, dwr1, q1, rz1a, rz2a, xs1, rx1,
-    dws0, dwr0, q0, rz1b, rz2b, xs0, rx0, rxx,
+    dws0, dwr0, q0, rz1b, rz2b, xs0, rx0,
     ssem, rsem, lsem,
 ):
     xl, y, xh, z, c = (lax.axis_index(a) for a in AXES)
@@ -381,19 +381,38 @@
                 value = value + rb[term, rows, self.cs].astype(F32)
             sb[k, rows, self.cs] = value.astype(BF16)
 
-        def make_all(self):
+        def first(self):
             self.make(0)
             self.s1 = [self.push(0, self.lo, x_peer), self.push(0, self.hi, x_peer)]
-            for k in range(1, 7):
-                self.make(k)
+
+        def make_rest(self):
+            self.make(5)
+            self.make(6)
             own[self.rows, self.cs] = self.piece(g)
 
-        def push_y(self):
+        def push_two(self):
             for i, rows in enumerate((self.lo, self.hi)):
                 self.push(1, rows, y_up, self.s2[i].sem)
                 self.push(2, rows, y_down, self.s2[i].sem)
+
+        def push_plain(self):
             self.push(3, self.hi, y_up, self.last.sem)
             self.push(4, self.lo, y_down, self.last.sem)
+
+        def rest(self):
+            self.make(1)
+            self.make(2)
+            self.push_two()
+            self.make(3)
+            self.make(4)
+            self.push_plain()
+            self.make_rest()
+
+        def prepare(self):
+            self.first()
+            for k in range(1, 5):
+                self.make(k)
+            self.make_rest()
 
         def mid1(self):
             self.s1[0].wait_recv()
@@ -537,27 +556,6 @@
             every = self.ds(self.all)
             self.xs[self.all, :] = self.z_sum(0).astype(BF16)
             self.h = send(self.xs.at[every, :], self.rx.at[every, :], h_peer, self.out)
-
-        def x_open(self):
-            self.give(0, 4)
-            self.keep(0, 2)
-            self.x_push(0)
-            self.keep(2, 4)
-            self.x_push(2)
-            self.give(4, 8)
-            self.keep(6, 8)
-            self.x_push(6)
-            self.keep(4, 6)
-            self.x_push(4)
-
-        def x_push(self, i):
-            every = self.ds(self.all)
-            self.st["x", i] = send(self.q.at[i, every, :], rxx.at[i // 2], h_peer, self.out)
-
-        def x_take(self, i):
-            self.st["x", i].wait_recv()
-            value = self.q[i + 1, self.all, :].astype(F32) + rxx[i // 2].astype(F32)
-            self.q[i + 1, self.all, :] = value.astype(BF16)
 
         def result(self):
             value = self.z_sum(1)
@@ -638,8 +636,6 @@
     blocks(1, CH, CH, 5, 8, False)
     activate(CH, CH, into_x2, slope1)
     head_b = head_send(1)
-    x_fwd1(c0)
-    x_fwd2(c0)
 
     da1, da2 = Scatter(0, CH, 0, CH), Scatter(0, CH, CH, CH)
     db1, db2 = Scatter(CH, CH, 0, CH), Scatter(CH, CH, CH, CH)
@@ -648,74 +644,84 @@
     g0a = Weights(0, pg0t, bufs0, 0, CH, 0)
     g0b = Weights(0, pg0t, bufs0, CH, CH, 0)
     head_loss(0, head_a)
-    da1.make_all()
-    da1.push_y()
-    da2.make_all()
-    da2.push_y()
+    da1.first()
+    da1.rest()
+    x_fwd1(c0)
+    da2.prepare()
     head_loss(1, head_b)
-    db1.make_all()
-    db1.push_y()
-    da1.mid1()
+    db1.first()
     hgp[...] = tn(x2[0:TR, :], og_r[...])
     g1.give(0, 4)
+    db1.rest()
     g1.keep(0, 2)
     g1.z_first()
+    da1.mid1()
     da1.mid2()
+    g1.give(4, 8)
+    db2.prepare()
     db1.mid1()
-    x_fwd3(c0)
-    da2.mid1()
-    db2.make_all()
-    db2.push_y()
-    da1.mid3()
+    x_fwd2(c0)
+    g1.keep(2, 4)
     db1.mid2()
-    g1.give(4, 8)
-    da2.mid2()
-    g1.keep(2, 4)
-    db1.mid3()
-    db2.mid1()
     g1.keep(6, 8)
     g1.z_plain()
-    da2.mid3()
+    da1.mid3()
     g1.keep(4, 6)
-    db2.mid2()
+    db1.mid3()
+    da2.mid1()
+    db2.mid1()
+    da2.push_two()
+    db2.push_two()
+    da2.push_plain()
+    db2.push_plain()
+    x_fwd3(c0)
     g1.z_added()
     da1.close()
+    db1.close()
+    g0a.give(0, 4)
+    g0a.keep(0, 2)
+    g0a.z_first()
+    da2.mid3()
+    db2.mid3()
+    g0a.give(4, 8)
     x_near(c0)
     x_far(c0)
     blocks(0, TR, AR, 1, 8, True)
     activate(TR, AR, into_x1, None)
-    db1.close()
-    g0a.give(0, 4)
-    db2.mid3()
+    da2.mid2()
+    g0a.keep(2, 4)
+    g0a.keep(6, 8)
+    g0a.z_plain()
+    db2.mid2()
     c1 = x_start(1, TR, AR)
     x_own(c1, "lo")
     x_own(c1, "hi")
-    g0a.keep(0, 2)
-    g0a.z_first()
-    g0a.give(4, 8)
-    g0a.late()
+    g0a.keep(4, 6)
+    g0a.z_added()
+    g1.cross()
     da2.close()
+    db2.close()
+    g0b.give(0, 4)
     x_fwd1(c1)
     x_fwd2(c1)
-    db2.close()
-    g0b.early()
-    g0a.z_added()
+    g0b.keep(0, 2)
+    g0b.z_first()
+    g0b.give(4, 8)
+    g0b.late()
     x_fwd3(c1)
-    g0b.late()
-    g1.cross()
+    g0b.z_added()
+    g0a.cross()
     x_near(c1)
     x_far(c1)
     blocks(1, TR, AR, 1, 8, True)
     activate(TR, AR, into_x2, None)
     ha_s[...] = nt(headt[0:32, :], x2[TR : TR + AR, :])[0:24, :]
     acts = to_group(ha_s, ha_r, ha_r.at[pl.ds(0, 7), :, :])
-    g0a.cross()
-    g0b.z_added()
+    g0b.cross()
     g1.result()
+    g0a.result()
     acts.wait_recv()
     al_out[...] = from_group(ha_s, ha_r)[0:ACT, :]
-    g0b.cross()
-    g0a.result()
     g0b.result()
 
     for view, sem in sends:
@@ -738,7 +744,7 @@
         v((2, 24, CH), F32), v((2, 8, 24, CH), F32), v((24, 128), F32), v((8, 24, 128), F32),
         v((TR, 128), BF16), v((TR, FB), BF16), v((FB, TR), BF16), v((FB, TR), BF16), v((FB, 128), F32),
         v((7, TR, FB), BF16), v((7, TR, FB), BF16), v((TR, FB), F32),
-        *dw_bufs(ER), *dw_bufs(FB), v((4, CH, WB), BF16),
+        *dw_bufs(ER), *dw_bufs(FB),
         pltpu.SemaphoreType.DMA((N_SEND,)), pltpu.SemaphoreType.DMA((N_RECV,)), pltpu.SemaphoreType.DMA((4,)),
     ]
     hbm = pl.BlockSpec(memory_space=pltpu.HBM)

time: 139 us -> 134 us (0.964)
  Pallas kernels: 134 us -> 129 us
    pallas_call x1, Pallas kernels: 134 us -> 129 us  [per_device(): pl.pallas_call(kernel, out_shape=(jax.ShapeDtypeStruct((2, WB, FB), F32),...]
where the time goes in v4:
time: 134 us
  Pallas kernels  129 us (96%)
  local copies, waits for them, and re-layouts  3.58 us (3%)
    pallas_call x1, Pallas kernels, per_device(): pl.pallas_call(kernel, out_shape=(jax.ShapeDtypeStruct((2, WB, FB), F32),...  129 us
    unnamed x7, local copies, waits for them, and re-layouts  3.58 us

profile of v4, /device:TPU:0, one launch (start us, length us, event | category | flops | bytes accessed | tf_op | source)
XLA Modules:
  0.0 133.5 jit_solution(17196997178978049504)
XLA Ops:
  0.6 129.3 %learner_step.1 = (f32[2,256,512]{2,1,0:T(8,128)}, f32[19,32]{1,0:T(8,128)}, f32[18,128]{1,0:T(8,128)}) custom-call(bf16[512,512]{1,0:T(8,128)(2,1)} %bitcast.5, bf16[128,512]{1,0:T(8,128)(2,1)} %nxt.1, bf16[2,256,512]{2,1,0:T(8,128)(2,1)} %wts.1, bf16[19,512]{1,0:T(8,128)(2,1)} %bitcast.7, f32[18,8,63]{2,1,0:T(8,128)} %bitcast.6, s32[8,63]{1,0:T(8,128)} %actions.1, ...), custom_call_target="tpu_custom_call" | custom-call | tf_op jit(solution)/shard_map/learner_step/pallas_call | solution.py:752
  129.9 0.0 copy-start.1
  129.9 2.3 %copy.14 = f32[2,256,512]{2,1,0:T(8,128)} copy(f32[2,256,512]{2,1,0:T(8,128)} %get-tuple-element.12) | data formatting | bytes 2097152
  132.2 0.0 copy-done.1
  132.2 0.0 copy-start
  132.2 0.6 copy.15
  132.8 0.1 copy-done
  132.9 0.6 copy.16
Async XLA Ops:
  129.9 2.3 %copy-start.1 = (f32[19,32]{1,0:T(8,128)S(1)}, f32[19,32]{1,0:T(8,128)}, u32[]{:S(2)}) copy-start(f32[19,32]{1,0:T(8,128)} %get-tuple-element.7) | copy-start | bytes 7300
  132.2 0.7 copy-start

commit v5 on v4

--- a/solution.py
+++ b/solution.py
@@ -85,14 +85,14 @@
 
 
 def kernel(
-    obs, nxt, wts, head, acting, actions, rewards, finished,
+    obs, nxt, wts, head_in, acting_in, actions_in, rewards_in, finished_in,
     dw_out, hg_out, al_out,
     xf0, xf1, wf0, wf1, acc, slope0, slope1, x2, headt, tmp, misc,
     hs, hr, ha_s, ha_r, og_r, pg1, pg1t, pg0t, hgp,
     sb, rb, own,
     dws1, dwr1, q1, rz1a, rz2a, xs1, rx1,
     dws0, dwr0, q0, rz1b, rz2b, xs0, rx0,
-    ssem, rsem, lsem,
+    dwv, hgv, alv, head, acting, actions, rewards, finished, ssem, rsem, lsem,
 ):
     xl, y, xh, z, c = (lax.axis_index(a) for a in AXES)
     g = xl * 4 + y
@@ -148,15 +148,23 @@
         pltpu.make_async_copy(wts.at[0], wf0.at[wg, pl.ds(cb, WB), :], lsem.at[1]),
         pltpu.make_async_copy(wts.at[1], wf1.at[wg, pl.ds(cb, WB), :], lsem.at[2]),
         pltpu.make_async_copy(nxt, xf0.at[g, pl.ds(TR, AR), :], lsem.at[3]),
+        pltpu.make_async_copy(head_in, head, lsem.at[4]),
+        pltpu.make_async_copy(acting_in, acting, lsem.at[5]),
+        pltpu.make_async_copy(actions_in, actions, lsem.at[6]),
+        pltpu.make_async_copy(rewards_in, rewards, lsem.at[7]),
+        pltpu.make_async_copy(finished_in, finished, lsem.at[8]),
     ]
     for load in loads:
         load.start()
 
+    stores = []
+
+    def store(src, dst):
+        stores.append(pltpu.make_async_copy(src, dst, lsem.at[9 + len(stores)]))
+        stores[-1].start()
+
     barrier = pltpu.get_barrier_semaphore()
-    friends = [h_peer, z_up, z_down, sibling]
-    for k in range(1, 8):
-        gt = (g + k) % 8
-        friends.append({"xl": gt // 4, "y": gt % 4})
+    friends = [x_peer, y_up, y_down, h_peer, z_up, z_down, sibling]
     for friend in friends:
         pl.semaphore_signal(barrier, inc=1, device_id=friend, device_id_type=MESH)
     pl.semaphore_wait(barrier, len(friends))
@@ -522,12 +530,6 @@
                 self.go(6 + xr, self.high, self.rz2.at[xr, 0], z_up, self.sums[xr].sem)
                 self.go(2 + xr, self.low, self.rz2.at[xr, 1], z_down, self.sums[xr].sem)
 
-        def early(self):
-            self.give(0, 4)
-            self.keep(0, 2)
-            self.z_first()
-            self.give(4, 8)
-
         def late(self):
             self.keep(2, 4)
             self.keep(6, 8)
@@ -562,9 +564,12 @@
             if 0 in self.halves:
                 self.h.wait_recv()
                 value = value + self.rx[self.all, :].astype(F32)
-            dw_out[self.layer, :, self.cs] = value[0 : self.cols, :].T
+            dwv[self.layer, :, self.cs] = value[0 : self.cols, :].T
+            where = (self.layer, slice(None), self.ds(self.cs))
+            store(dwv.at[where], dw_out.at[where])
             if self.extra:
-                hg_out[...] = value[self.cols :, 0:128].T[0 : ACT + 1, :]
+                hgv[...] = value[self.cols :, 0:128].T[0 : ACT + 1, :]
+                store(hgv, hg_out)
 
     loads[0].wait()
     loads[1].wait()
@@ -574,8 +579,8 @@
     x_own(a0, "hi")
     x_own(b0, "lo")
     x_own(b0, "hi")
-    loads[2].wait()
-    loads[3].wait()
+    for load in loads[2:]:
+        load.wait()
 
     headt[...] = jnp.zeros_like(headt)
     headt[0 : ACT + 1, :] = head[...]
@@ -651,16 +656,17 @@
     head_loss(1, head_b)
     db1.first()
     hgp[...] = tn(x2[0:TR, :], og_r[...])
-    g1.give(0, 4)
+    g1.give(0, 2)
     db1.rest()
     g1.keep(0, 2)
     g1.z_first()
     da1.mid1()
     da1.mid2()
-    g1.give(4, 8)
+    g1.give(2, 8)
     db2.prepare()
     db1.mid1()
     x_fwd2(c0)
+    x_fwd3(c0)
     g1.keep(2, 4)
     db1.mid2()
     g1.keep(6, 8)
@@ -674,20 +680,19 @@
     db2.push_two()
     da2.push_plain()
     db2.push_plain()
-    x_fwd3(c0)
     g1.z_added()
+    x_near(c0)
+    x_far(c0)
+    blocks(0, TR, AR, 1, 8, True)
+    activate(TR, AR, into_x1, None)
     da1.close()
     db1.close()
-    g0a.give(0, 4)
+    g0a.give(0, 2)
     g0a.keep(0, 2)
     g0a.z_first()
     da2.mid3()
     db2.mid3()
-    g0a.give(4, 8)
-    x_near(c0)
-    x_far(c0)
-    blocks(0, TR, AR, 1, 8, True)
-    activate(TR, AR, into_x1, None)
+    g0a.give(2, 8)
     da2.mid2()
     g0a.keep(2, 4)
     g0a.keep(6, 8)
@@ -701,34 +706,68 @@
     g1.cross()
     da2.close()
     db2.close()
-    g0b.give(0, 4)
+    g0b.give(0, 2)
+    g0b.keep(0, 2)
+    g0b.z_first()
     x_fwd1(c1)
     x_fwd2(c1)
-    g0b.keep(0, 2)
-    g0b.z_first()
-    g0b.give(4, 8)
+    g0b.give(2, 8)
     g0b.late()
     x_fwd3(c1)
+    x_near(c1)
+    blocks(1, TR, AR, 1, 5, True)
     g0b.z_added()
     g0a.cross()
-    x_near(c1)
     x_far(c1)
-    blocks(1, TR, AR, 1, 8, True)
+    g0b.cross()
+    blocks(1, TR, AR, 5, 8, False)
     activate(TR, AR, into_x2, None)
     ha_s[...] = nt(headt[0:32, :], x2[TR : TR + AR, :])[0:24, :]
     acts = to_group(ha_s, ha_r, ha_r.at[pl.ds(0, 7), :, :])
-    g0b.cross()
     g1.result()
     g0a.result()
     acts.wait_recv()
-    al_out[...] = from_group(ha_s, ha_r)[0:ACT, :]
+    alv[...] = from_group(ha_s, ha_r)[0:ACT, :]
+    store(alv, al_out)
     g0b.result()
 
+    for copy in stores:
+        copy.wait()
     for view, sem in sends:
         pltpu.make_async_remote_copy(
             src_ref=view, dst_ref=view, send_sem=sem, recv_sem=rsem.at[0], device_id=x_peer, device_id_type=MESH,
         ).wait_send()
     assert (count[0], count[1]) == (N_RECV, N_SEND), count
+
+
+def hand_out_kernel(dw, hg, al, dw_out, hg_out, al_out, dwv, hgv, alv, isem, osem):
+    views = [(dw.at[p], dwv.at[p], dw_out.at[p]) for p in range(dw.shape[0])]
+    views += [(hg, hgv, hg_out), (al, alv, al_out)]
+    loads = [pltpu.make_async_copy(a, b, isem.at[i]) for i, (a, b, _) in enumerate(views)]
+    stores = [pltpu.make_async_copy(b, o, osem.at[i]) for i, (_, b, o) in enumerate(views)]
+    for copy in loads:
+        copy.start()
+    for load, copy in zip(loads, stores):
+        load.wait()
+        copy.start()
+    for copy in stores:
+        copy.wait()
+
+
+def hand_out(dw, hg, al):
+    parts = dw.reshape(4, WB // 2, FB)
+    arrays = (parts, hg, al)
+    hbm = pl.BlockSpec(memory_space=pltpu.HBM)
+    moved, hg, al = pl.pallas_call(
+        hand_out_kernel,
+        out_shape=tuple(jax.ShapeDtypeStruct(a.shape, a.dtype) for a in arrays),
+        in_specs=[hbm] * 3,
+        out_specs=(hbm,) * 3,
+        scratch_shapes=[pltpu.VMEM(a.shape, a.dtype) for a in arrays]
+        + [pltpu.SemaphoreType.DMA((6,)), pltpu.SemaphoreType.DMA((6,))],
+        name="hand_out",
+    )(*arrays)
+    return moved.reshape(dw.shape), hg, al
 
 
 def per_device(observations, next_observations, trunk_weights, head_weights, acting, actions, rewards, finished):
@@ -745,10 +784,12 @@
         v((TR, 128), BF16), v((TR, FB), BF16), v((FB, TR), BF16), v((FB, TR), BF16), v((FB, 128), F32),
         v((7, TR, FB), BF16), v((7, TR, FB), BF16), v((TR, FB), F32),
         *dw_bufs(ER), *dw_bufs(FB),
-        pltpu.SemaphoreType.DMA((N_SEND,)), pltpu.SemaphoreType.DMA((N_RECV,)), pltpu.SemaphoreType.DMA((4,)),
+        v((2, WB, FB), F32), v((ACT + 1, 32), F32), v((ACT, AR), F32),
+        v((ACT + 1, FB), BF16), v((ACT, 8, STEPS - 1), F32), v((8, STEPS - 1), jnp.int32), v((8, STEPS - 1), F32),
+        v((8, STEPS - 1), jnp.int32),
+        pltpu.SemaphoreType.DMA((N_SEND,)), pltpu.SemaphoreType.DMA((N_RECV,)), pltpu.SemaphoreType.DMA((14,)),
     ]
     hbm = pl.BlockSpec(memory_space=pltpu.HBM)
-    vmem = pl.BlockSpec(memory_space=pltpu.VMEM)
     trunk_grads, head_grads, actor_logits = pl.pallas_call(
         kernel,
         out_shape=(
@@ -756,8 +797,8 @@
             jax.ShapeDtypeStruct((ACT + 1, 32), F32),
             jax.ShapeDtypeStruct((ACT, AR), F32),
         ),
-        in_specs=[hbm, hbm, hbm, vmem, vmem, vmem, vmem, vmem],
-        out_specs=(vmem, vmem, vmem),
+        in_specs=[hbm] * 8,
+        out_specs=(hbm, hbm, hbm),
         scratch_shapes=scratch,
         compiler_params=pltpu.CompilerParams(
             collective_id=0, has_side_effects=True, vmem_limit_bytes=62 * 1024 * 1024
@@ -767,6 +808,7 @@
         observations.reshape(TR, FB), next_observations, trunk_weights, head_weights.T, acting.transpose(2, 0, 1),
         actions, rewards, finished,
     )
+    trunk_grads, head_grads, actor_logits = hand_out(trunk_grads, head_grads, actor_logits)
     return trunk_grads, head_grads.T, actor_logits.T
 
 

time: 134 us -> 129 us (0.963)
  local copies, waits for them, and re-layouts: 3.58 us -> 0 us
    unnamed x7 -> x0, local copies, waits for them, and re-layouts: 3.58 us -> none
    pallas_call x1, Pallas kernels: 129 us -> 126 us  [per_device(): pl.pallas_call(kernel, out_shape=(jax.ShapeDtypeStruct((2, WB, FB), F32),...]
    pallas_call x0 -> x1, Pallas kernels: none -> 2.02 us  [hand_out(): pl.pallas_call(hand_out_kernel, out_shape=tuple((jax.ShapeDtypeStruct(a.s...]
where the time goes in v5:
time: 129 us
  Pallas kernels  128 us (99%)
    pallas_call x1, Pallas kernels, per_device(): pl.pallas_call(kernel, out_shape=(jax.ShapeDtypeStruct((2, WB, FB), F32),...  126 us

profile of v5, /device:TPU:0, one launch (start us, length us, event | category | flops | bytes accessed | tf_op | source)
XLA Modules:
  0.0 128.6 jit_solution(11262950283119561974)
XLA Ops:
  0.6 125.9 %learner_step.1 = (f32[2,256,512]{2,1,0:T(8,128)}, f32[19,32]{1,0:T(8,128)}, f32[18,128]{1,0:T(8,128)}) custom-call(bf16[512,512]{1,0:T(8,128)(2,1)} %bitcast.8, bf16[128,512]{1,0:T(8,128)(2,1)} %nxt.1, bf16[2,256,512]{2,1,0:T(8,128)(2,1)} %wts.1, bf16[19,512]{1,0:T(8,128)(2,1)} %bitcast.10, f32[18,8,63]{2,1,0:T(8,128)} %bitcast.9, s32[8,63]{1,0:T(8,128)} %actions_in.1, ...), custom_call_target="tpu_custom_call" | custom-call | tf_op jit(solution)/shard_map/learner_step/pallas_call | solution.py:793
  126.5 2.0 %hand_out.1 = (f32[4,128,512]{2,1,0:T(8,128)}, f32[19,32]{1,0:T(8,128)}, f32[18,128]{1,0:T(8,128)}) custom-call(f32[4,128,512]{2,1,0:T(8,128)} %bitcast.7, f32[19,32]{1,0:T(8,128)} %get-tuple-element.10.hg, f32[18,128]{1,0:T(8,128)} %get-tuple-element.11.al), custom_call_target="tpu_custom_call" | custom-call | tf_op jit(solution)/shard_map/hand_out/pallas_call | solution.py:761

commit v6 on v5

--- a/solution.py
+++ b/solution.py
@@ -92,7 +92,7 @@
     sb, rb, own,
     dws1, dwr1, q1, rz1a, rz2a, xs1, rx1,
     dws0, dwr0, q0, rz1b, rz2b, xs0, rx0,
-    dwv, hgv, alv, head, acting, actions, rewards, finished, ssem, rsem, lsem,
+    head, acting, actions, rewards, finished, ssem, rsem, lsem,
 ):
     xl, y, xh, z, c = (lax.axis_index(a) for a in AXES)
     g = xl * 4 + y
@@ -156,12 +156,6 @@
     ]
     for load in loads:
         load.start()
-
-    stores = []
-
-    def store(src, dst):
-        stores.append(pltpu.make_async_copy(src, dst, lsem.at[9 + len(stores)]))
-        stores[-1].start()
 
     barrier = pltpu.get_barrier_semaphore()
     friends = [x_peer, y_up, y_down, h_peer, z_up, z_down, sibling]
@@ -564,12 +558,9 @@
             if 0 in self.halves:
                 self.h.wait_recv()
                 value = value + self.rx[self.all, :].astype(F32)
-            dwv[self.layer, :, self.cs] = value[0 : self.cols, :].T
-            where = (self.layer, slice(None), self.ds(self.cs))
-            store(dwv.at[where], dw_out.at[where])
+            dw_out[self.layer, :, self.cs] = value[0 : self.cols, :].T
             if self.extra:
-                hgv[...] = value[self.cols :, 0:128].T[0 : ACT + 1, :]
-                store(hgv, hg_out)
+                hg_out[...] = value[self.cols :, 0:128].T[0 : ACT + 1, :]
 
     loads[0].wait()
     loads[1].wait()
@@ -714,25 +705,22 @@
     g0b.give(2, 8)
     g0b.late()
     x_fwd3(c1)
+    g0b.z_added()
+    g0a.cross()
     x_near(c1)
     blocks(1, TR, AR, 1, 5, True)
-    g0b.z_added()
-    g0a.cross()
     x_far(c1)
-    g0b.cross()
     blocks(1, TR, AR, 5, 8, False)
     activate(TR, AR, into_x2, None)
     ha_s[...] = nt(headt[0:32, :], x2[TR : TR + AR, :])[0:24, :]
     acts = to_group(ha_s, ha_r, ha_r.at[pl.ds(0, 7), :, :])
+    g0b.cross()
     g1.result()
     g0a.result()
     acts.wait_recv()
-    alv[...] = from_group(ha_s, ha_r)[0:ACT, :]
-    store(alv, al_out)
+    al_out[...] = from_group(ha_s, ha_r)[0:ACT, :]
     g0b.result()
 
-    for copy in stores:
-        copy.wait()
     for view, sem in sends:
         pltpu.make_async_remote_copy(
             src_ref=view, dst_ref=view, send_sem=sem, recv_sem=rsem.at[0], device_id=x_peer, device_id_type=MESH,
@@ -740,34 +728,25 @@
     assert (count[0], count[1]) == (N_RECV, N_SEND), count
 
 
-def hand_out_kernel(dw, hg, al, dw_out, hg_out, al_out, dwv, hgv, alv, isem, osem):
-    views = [(dw.at[p], dwv.at[p], dw_out.at[p]) for p in range(dw.shape[0])]
-    views += [(hg, hgv, hg_out), (al, alv, al_out)]
-    loads = [pltpu.make_async_copy(a, b, isem.at[i]) for i, (a, b, _) in enumerate(views)]
-    stores = [pltpu.make_async_copy(b, o, osem.at[i]) for i, (_, b, o) in enumerate(views)]
-    for copy in loads:
+def hand_out_kernel(dw, hg, al, dw_out, hg_out, al_out, sems):
+    copies = [pltpu.make_async_copy(a, b, sems.at[i]) for i, (a, b) in enumerate(((dw, dw_out), (hg, hg_out), (al, al_out)))]
+    for copy in copies:
         copy.start()
-    for load, copy in zip(loads, stores):
-        load.wait()
-        copy.start()
-    for copy in stores:
+    for copy in copies:
         copy.wait()
 
 
-def hand_out(dw, hg, al):
-    parts = dw.reshape(4, WB // 2, FB)
-    arrays = (parts, hg, al)
+def hand_out(*arrays):
+    arrays = [pltpu.with_memory_space_constraint(a, pltpu.VMEM) for a in arrays]
     hbm = pl.BlockSpec(memory_space=pltpu.HBM)
-    moved, hg, al = pl.pallas_call(
+    return pl.pallas_call(
         hand_out_kernel,
         out_shape=tuple(jax.ShapeDtypeStruct(a.shape, a.dtype) for a in arrays),
-        in_specs=[hbm] * 3,
+        in_specs=[pl.BlockSpec(memory_space=pltpu.VMEM)] * 3,
         out_specs=(hbm,) * 3,
-        scratch_shapes=[pltpu.VMEM(a.shape, a.dtype) for a in arrays]
-        + [pltpu.SemaphoreType.DMA((6,)), pltpu.SemaphoreType.DMA((6,))],
+        scratch_shapes=[pltpu.SemaphoreType.DMA((3,))],
         name="hand_out",
     )(*arrays)
-    return moved.reshape(dw.shape), hg, al
 
 
 def per_device(observations, next_observations, trunk_weights, head_weights, acting, actions, rewards, finished):
@@ -784,24 +763,24 @@
         v((TR, 128), BF16), v((TR, FB), BF16), v((FB, TR), BF16), v((FB, TR), BF16), v((FB, 128), F32),
         v((7, TR, FB), BF16), v((7, TR, FB), BF16), v((TR, FB), F32),
         *dw_bufs(ER), *dw_bufs(FB),
-        v((2, WB, FB), F32), v((ACT + 1, 32), F32), v((ACT, AR), F32),
         v((ACT + 1, FB), BF16), v((ACT, 8, STEPS - 1), F32), v((8, STEPS - 1), jnp.int32), v((8, STEPS - 1), F32),
         v((8, STEPS - 1), jnp.int32),
-        pltpu.SemaphoreType.DMA((N_SEND,)), pltpu.SemaphoreType.DMA((N_RECV,)), pltpu.SemaphoreType.DMA((14,)),
+        pltpu.SemaphoreType.DMA((N_SEND,)), pltpu.SemaphoreType.DMA((N_RECV,)), pltpu.SemaphoreType.DMA((9,)),
     ]
     hbm = pl.BlockSpec(memory_space=pltpu.HBM)
+    vm = pl.BlockSpec(memory_space=pltpu.VMEM)
     trunk_grads, head_grads, actor_logits = pl.pallas_call(
         kernel,
         out_shape=(
-            jax.ShapeDtypeStruct((2, WB, FB), F32),
-            jax.ShapeDtypeStruct((ACT + 1, 32), F32),
-            jax.ShapeDtypeStruct((ACT, AR), F32),
+            pltpu.VMEM((2, WB, FB), F32),
+            pltpu.VMEM((ACT + 1, 32), F32),
+            pltpu.VMEM((ACT, AR), F32),
         ),
         in_specs=[hbm] * 8,
-        out_specs=(hbm, hbm, hbm),
+        out_specs=(vm,) * 3,
         scratch_shapes=scratch,
         compiler_params=pltpu.CompilerParams(
-            collective_id=0, has_side_effects=True, vmem_limit_bytes=62 * 1024 * 1024
+            collective_id=0, has_side_effects=True, vmem_limit_bytes=58 * 1024 * 1024
         ),
         name="learner_step",
     )(

time: 129 us -> 127 us (0.984)
  Pallas kernels: 128 us -> 126 us
where the time goes in v6:
time: 127 us
  Pallas kernels  126 us (99%)
    pallas_call x1, Pallas kernels, per_device(): pl.pallas_call(kernel, out_shape=(pltpu.VMEM((2, WB, FB), F32), pltpu.VME...  125 us

profile of v6, /device:TPU:0, one launch (start us, length us, event | category | flops | bytes accessed | tf_op | source)
XLA Modules:
  0.0 126.5 jit_solution(11989444100038499664)
XLA Ops:
  0.6 124.9 %learner_step.1 = (f32[2,256,512]{2,1,0:T(8,128)S(1)}, f32[19,32]{1,0:T(8,128)S(1)}, f32[18,128]{1,0:T(8,128)S(1)}) custom-call(bf16[512,512]{1,0:T(8,128)(2,1)} %bitcast.5, bf16[128,512]{1,0:T(8,128)(2,1)} %nxt.1, bf16[2,256,512]{2,1,0:T(8,128)(2,1)} %wts.1, bf16[19,512]{1,0:T(8,128)(2,1)} %bitcast.7, f32[18,8,63]{2,1,0:T(8,128)} %bitcast.6, ...), custom_call_target="tpu_custom_call" | custom-call | tf_op jit(solution)/shard_map/learner_step/pallas_call | solution.py:772
  125.5 1.0 hand_out.1

commit v7 on v6

--- a/solution.py
+++ b/solution.py
@@ -28,7 +28,7 @@
 STEPS = 64
 ACT = 18
 ER = 544
-N_RECV, N_SEND = 148, 21
+N_RECV, N_SEND = 112, 21
 CH = 256
 
 
@@ -172,27 +172,26 @@
         def go(block, rows, device, recv_sem=None):
             return send(buf.at[block, rows, :], buf.at[block, rows, :], device, out, recv_sem)
 
-        near = Recv(new_recv(), buf.at[0, pl.ds(0, amount), :])
+        near, first_two, passed = (Recv(new_recv(), buf.at[0, pl.ds(0, amount), :]) for _ in range(3))
         far = Recv(new_recv(), buf.at[pl.ds(0, 3), pl.ds(0, amount), :])
-        return {"go": go, "lo": lo, "hi": hi, "near": near, "far": far}
+        return {"go": go, "lo": lo, "hi": hi, "near": near, "far": far, "two": first_two, "f": passed}
 
     def x_own(st, rows):
         go, lo = st["go"], st["lo"]
         if rows == "lo":
-            st["up_lo"] = go(g, lo, y_up)
+            go(g, lo, y_up, st["two"].sem)
             st["x_lo"] = go(g, lo, x_peer)
         else:
-            st["dn_hi"] = go(g, st["hi"], y_down)
+            go(g, st["hi"], y_down, st["two"].sem)
             st["x_hi"] = go(g, st["hi"], x_peer)
             go(g, st["hi"], y_up, st["near"].sem)
             go(g, lo, y_down, st["near"].sem)
 
     def x_fwd1(st):
         go = st["go"]
-        st["up_lo"].wait_recv()
-        st["f_lo"] = go(rel_g(0, 3), st["lo"], y_up)
-        st["dn_hi"].wait_recv()
-        st["f_hi"] = go(rel_g(0, 1), st["hi"], y_down)
+        st["two"].wait_recv()
+        go(rel_g(0, 3), st["lo"], y_up, st["f"].sem)
+        go(rel_g(0, 1), st["hi"], y_down, st["f"].sem)
 
     def x_fwd2(st):
         go, block, far = st["go"], rel_g(1, 0), st["far"].sem
@@ -205,9 +204,8 @@
 
     def x_fwd3(st):
         go, block, far = st["go"], rel_g(0, 2), st["far"].sem
-        st["f_lo"].wait_recv()
+        st["f"].wait_recv()
         go(block, st["lo"], x_peer, far)
-        st["f_hi"].wait_recv()
         go(block, st["hi"], x_peer, far)
 
     def x_near(st):
@@ -234,14 +232,14 @@
             return send(buf.at[where], buf.at[where], device, out, recv_sem)
 
         st = {"go": go}
-        st["f"] = Recv(new_recv(), buf.at[0, pl.ds(0, WB), :])
-        st["g"] = Recv(new_recv(), buf.at[0, pl.ds(0, WB), :])
+        for name in ("f", "g", "two", "others", "h_two", "h_others"):
+            st[name] = Recv(new_recv(), buf.at[0, pl.ds(0, WB), :])
         st["sib"] = Recv(new_recv(), buf.at[pl.ds(0, 4), :, :])
-        st["up_lo"] = go(wg, "lo", z_up)
-        st["dn_hi"] = go(wg, "hi", z_down)
+        go(wg, "lo", z_up, st["two"].sem)
+        go(wg, "hi", z_down, st["two"].sem)
         st["h"] = go(wg, "all", h_peer)
-        st["up_hi"] = go(wg, "hi", z_up)
-        st["dn_lo"] = go(wg, "lo", z_down)
+        go(wg, "hi", z_up, st["others"].sem)
+        go(wg, "lo", z_down, st["others"].sem)
         w_share(st, wg)
         return st
 
@@ -250,37 +248,33 @@
 
     def w_fwd1(st):
         go = st["go"]
-        st["up_lo"].wait_recv()
+        st["two"].wait_recv()
         go(rel_w(0, 3), "lo", z_up, st["f"].sem)
-        st["dn_hi"].wait_recv()
         go(rel_w(0, 1), "hi", z_down, st["f"].sem)
 
     def w_fwd2(st):
         go, far = st["go"], rel_w(1, 0)
         st["h"].wait_recv()
-        st["h_up_lo"] = go(far, "lo", z_up)
-        st["h_dn_hi"] = go(far, "hi", z_down)
-        st["h_up_hi"] = go(far, "hi", z_up)
-        st["h_dn_lo"] = go(far, "lo", z_down)
+        go(far, "lo", z_up, st["h_two"].sem)
+        go(far, "hi", z_down, st["h_two"].sem)
+        go(far, "hi", z_up, st["h_others"].sem)
+        go(far, "lo", z_down, st["h_others"].sem)
         w_share(st, far)
-        st["up_hi"].wait_recv()
+        st["others"].wait_recv()
         w_share(st, rel_w(0, 3))
-        st["dn_lo"].wait_recv()
         w_share(st, rel_w(0, 1))
 
     def w_fwd3(st):
         go = st["go"]
-        st["h_up_lo"].wait_recv()
+        st["h_two"].wait_recv()
         go(rel_w(1, 3), "lo", z_up, st["g"].sem)
-        st["h_dn_hi"].wait_recv()
         go(rel_w(1, 1), "hi", z_down, st["g"].sem)
         st["f"].wait_recv()
         w_share(st, rel_w(0, 2))
 
     def w_finish(st):
-        st["h_up_hi"].wait_recv()
+        st["h_others"].wait_recv()
         w_share(st, rel_w(1, 3))
-        st["h_dn_lo"].wait_recv()
         w_share(st, rel_w(1, 1))
         st["g"].wait_recv()
         w_share(st, rel_w(1, 2))
@@ -362,6 +356,7 @@
             self.cs = slice(col, col + cols)
             self.out = new_send(sb.at[:, self.ds(self.rows), self.ds(self.cs)])
             self.s2 = [Recv(new_recv(), rb.at[pl.ds(0, 2), self.ds(rows), self.ds(self.cs)]) for rows in (self.lo, self.hi)]
+            self.s4 = Recv(new_recv(), rb.at[0, self.ds(self.rows), self.ds(self.cs)])
             self.last = Recv(new_recv(), rb.at[pl.ds(0, 3), self.ds(self.rows), self.ds(self.cs)])
 
         def ds(self, rows):
@@ -419,10 +414,10 @@
         def mid1(self):
             self.s1[0].wait_recv()
             self.add_in(5, self.lo, 0)
-            self.s4u = self.push(5, self.lo, y_up)
+            self.push(5, self.lo, y_up, self.s4.sem)
             self.s1[1].wait_recv()
             self.add_in(5, self.hi, 0)
-            self.s4d = self.push(5, self.hi, y_down)
+            self.push(5, self.hi, y_down, self.s4.sem)
 
         def mid2(self):
             for i, rows in enumerate((self.lo, self.hi)):
@@ -431,10 +426,9 @@
                 self.push(6, rows, x_peer, self.last.sem)
 
         def mid3(self):
-            self.s4u.wait_recv()
+            self.s4.wait_recv()
             self.add_in(3, self.lo, 5)
             self.push(3, self.lo, y_up, self.last.sem)
-            self.s4d.wait_recv()
             self.add_in(4, self.hi, 5)
             self.push(4, self.hi, y_down, self.last.sem)
 
@@ -456,7 +450,7 @@
             self.all, half = slice(col, col + self.size), col + cols // 2
             self.low, self.high = slice(col, half), slice(half, col + self.size)
             self.base = count[0]
-            count[0] += 8
+            count[0] += 4
             every = self.ds(self.all)
             self.out = new_send(self.q.at[pl.ds(0, 7), every, :])
             self.give_sem = new_send(self.dws.at[:, every, :])
@@ -473,7 +467,7 @@
             every = self.ds(self.all)
             return pltpu.make_async_remote_copy(
                 src_ref=self.dws.at[i, every, :], dst_ref=self.dwr.at[i, every, :],
-                send_sem=self.give_sem, recv_sem=rsem.at[self.base + i],
+                send_sem=self.give_sem, recv_sem=rsem.at[self.base + i // 2],
                 device_id=sibling, device_id_type=MESH,
             )
 
@@ -497,11 +491,12 @@
 
         def keep(self, i0, i1):
             q, dwr, cs, top = self.q, self.dwr, self.cs, self.top
+            assert i1 == i0 + 2
+            Recv(rsem.at[self.base + i0 // 2], dwr.at[pl.ds(i0, 2), self.ds(self.all), :]).wait_recv()
 
             def body(i, carry):
                 block = self.block(i)
                 term = nn(self.pgt[cs, :], xf[self.layer][block, 0:TR, pl.ds(cb, WB)])
-                self.copy_of(i).wait_recv()
                 q[i, cs, :] = (term + dwr[i, cs, :].astype(F32)).astype(BF16)
                 if self.extra:
                     q[i, top, 0:128] = (self.head_rows(block, c) + dwr[i, top, 0:128].astype(F32)).astype(BF16)

time: 127 us -> 126 us (level)
  no operation moved by 1% of the time
where the time goes in v7:
time: 126 us
  Pallas kernels  126 us (100%)
    pallas_call x1, Pallas kernels, per_device(): pl.pallas_call(kernel, out_shape=(pltpu.VMEM((2, WB, FB), F32), pltpu.VME...  125 us

profile of v7, /device:TPU:0, one launch (start us, length us, event | category | flops | bytes accessed | tf_op | source)
XLA Modules:
  0.0 126.3 jit_solution(12763562845541005273)
XLA Ops:
  0.6 124.7 %learner_step.1 = (f32[2,256,512]{2,1,0:T(8,128)S(1)}, f32[19,32]{1,0:T(8,128)S(1)}, f32[18,128]{1,0:T(8,128)S(1)}) custom-call(bf16[512,512]{1,0:T(8,128)(2,1)} %bitcast.5, bf16[128,512]{1,0:T(8,128)(2,1)} %nxt.1, bf16[2,256,512]{2,1,0:T(8,128)(2,1)} %wts.1, bf16[19,512]{1,0:T(8,128)(2,1)} %bitcast.7, f32[18,8,63]{2,1,0:T(8,128)} %bitcast.6, ...), custom_call_target="tpu_custom_call" | custom-call | tf_op jit(solution)/shard_map/learner_step/pallas_call | solution.py:767
  125.3 1.0 hand_out.1

commit v8 on v7

--- a/solution.py
+++ b/solution.py
@@ -28,7 +28,7 @@
 STEPS = 64
 ACT = 18
 ER = 544
-N_RECV, N_SEND = 112, 21
+N_RECV, N_SEND = 118, 21
 CH = 256
 
 
@@ -173,8 +173,9 @@
             return send(buf.at[block, rows, :], buf.at[block, rows, :], device, out, recv_sem)
 
         near, first_two, passed = (Recv(new_recv(), buf.at[0, pl.ds(0, amount), :]) for _ in range(3))
-        far = Recv(new_recv(), buf.at[pl.ds(0, 3), pl.ds(0, amount), :])
-        return {"go": go, "lo": lo, "hi": hi, "near": near, "far": far, "two": first_two, "f": passed}
+        side = Recv(new_recv(), buf.at[pl.ds(0, 2), pl.ds(0, amount), :])
+        far = Recv(new_recv(), buf.at[0, pl.ds(0, amount), :])
+        return {"go": go, "lo": lo, "hi": hi, "near": near, "side": side, "far": far, "two": first_two, "f": passed}
 
     def x_own(st, rows):
         go, lo = st["go"], st["lo"]
@@ -194,7 +195,7 @@
         go(rel_g(0, 1), st["hi"], y_down, st["f"].sem)
 
     def x_fwd2(st):
-        go, block, far = st["go"], rel_g(1, 0), st["far"].sem
+        go, block, far = st["go"], rel_g(1, 0), st["side"].sem
         st["x_lo"].wait_recv()
         go(block, st["lo"], y_up, far)
         go(block, st["lo"], y_down, far)
@@ -210,6 +211,9 @@
 
     def x_near(st):
         st["near"].wait_recv()
+
+    def x_side(st):
+        st["side"].wait_recv()
 
     def x_far(st):
         st["far"].wait_recv()
@@ -287,7 +291,9 @@
             acc[rows, :] = nn(buf[g, rows, :], weights[g])
 
         def body(j, carry):
-            block = ((xl + j // 4) % 2) * 4 + (y + j % 4) % 4
+            step = j % 4
+            step = step + (step // 2) * (5 - 2 * step)
+            block = ((xl + j // 4) % 2) * 4 + (y + step) % 4
             acc[rows, :] += nn(buf[block, rows, :], weights[block])
             return carry
 
@@ -593,14 +599,18 @@
     w_finish(w0)
     x_near(a0)
     blocks(0, 0, CH, 1, 5, True)
+    x_side(a0)
+    blocks(0, 0, CH, 5, 7, False)
     x_far(a0)
-    blocks(0, 0, CH, 5, 8, False)
+    blocks(0, 0, CH, 7, 8, False)
     a1 = next_layer(0, slope0)
     w_fwd1(w1)
     x_near(b0)
     blocks(0, CH, CH, 1, 5, True)
+    x_side(b0)
+    blocks(0, CH, CH, 5, 7, False)
     x_far(b0)
-    blocks(0, CH, CH, 5, 8, False)
+    blocks(0, CH, CH, 7, 8, False)
     b1 = next_layer(CH, slope0)
 
     x_fwd1(a1)
@@ -614,8 +624,10 @@
     w_finish(w1)
     x_near(a1)
     blocks(1, 0, CH, 1, 5, True)
+    x_side(a1)
+    blocks(1, 0, CH, 5, 7, False)
     x_far(a1)
-    blocks(1, 0, CH, 5, 8, False)
+    blocks(1, 0, CH, 7, 8, False)
     activate(0, CH, into_x2, slope1)
     head_a = head_send(0)
     c0 = x_start(0, TR, AR)
@@ -623,8 +635,10 @@
     x_own(c0, "hi")
     x_near(b1)
     blocks(1, CH, CH, 1, 5, True)
+    x_side(b1)
+    blocks(1, CH, CH, 5, 7, False)
     x_far(b1)
-    blocks(1, CH, CH, 5, 8, False)
+    blocks(1, CH, CH, 7, 8, False)
     activate(CH, CH, into_x2, slope1)
     head_b = head_send(1)
 
@@ -668,6 +682,7 @@
     db2.push_plain()
     g1.z_added()
     x_near(c0)
+    x_side(c0)
     x_far(c0)
     blocks(0, TR, AR, 1, 8, True)
     activate(TR, AR, into_x1, None)
@@ -704,8 +719,10 @@
     g0a.cross()
     x_near(c1)
     blocks(1, TR, AR, 1, 5, True)
+    x_side(c1)
+    blocks(1, TR, AR, 5, 7, False)
     x_far(c1)
-    blocks(1, TR, AR, 5, 8, False)
+    blocks(1, TR, AR, 7, 8, False)
     activate(TR, AR, into_x2, None)
     ha_s[...] = nt(headt[0:32, :], x2[TR : TR + AR, :])[0:24, :]
     acts = to_group(ha_s, ha_r, ha_r.at[pl.ds(0, 7), :, :])

time: 126 us -> 127 us (level)
  no operation moved by 1% of the time
where the time goes in v8:
time: 127 us; the launch traced here: 126 us
  Pallas kernels  126 us (99%)
    pallas_call x1, Pallas kernels, per_device(): pl.pallas_call(kernel, out_shape=(pltpu.VMEM((2, WB, FB), F32), pltpu.VME...  125 us

profile of v8, /device:TPU:0, one launch (start us, length us, event | category | flops | bytes accessed | tf_op | source)
XLA Modules:
  0.0 126.4 jit_solution(1617012383901316748)
XLA Ops:
  0.6 124.8 %learner_step.1 = (f32[2,256,512]{2,1,0:T(8,128)S(1)}, f32[19,32]{1,0:T(8,128)S(1)}, f32[18,128]{1,0:T(8,128)S(1)}) custom-call(bf16[512,512]{1,0:T(8,128)(2,1)} %bitcast.5, bf16[128,512]{1,0:T(8,128)(2,1)} %nxt.1, bf16[2,256,512]{2,1,0:T(8,128)(2,1)} %wts.1, bf16[19,512]{1,0:T(8,128)(2,1)} %bitcast.7, f32[18,8,63]{2,1,0:T(8,128)} %bitcast.6, ...), custom_call_target="tpu_custom_call" | custom-call | tf_op jit(solution)/shard_map/learner_step/pallas_call | solution.py:784
  125.4 1.0 hand_out.1
